TPU v7x, 256 devices: a whole 4x4x8 slice. The times are simulated.
256 devices in a mesh: band: 64 (over y, z, core), mp: 4 (over x).
Axes of the slice: x: 4, y: 4, z: 8, core: 2. Of those that a mesh axis runs over, the one named last changes fastest.
Arguments:
- grid_latent: bfloat16 [262144, 512], P('band'), may hold values from -6 to 6
- edge_latent: bfloat16 [393216, 512], P('band'), may hold values from -6 to 6
- mesh_latent: bfloat16 [40960, 512], P('band', 'mp'), may hold values from -6 to 6
- mesh_grad: bfloat16 [40960, 512], P('band', 'mp'), may hold values from -96 to 96
- counts: int32 [40960], P('band'), may hold values from 8 to 64
- request: int32 [64, 7, 128], P('band'), may hold values from -1 to 639, as said below
- edge_sender: int32 [393216], P('band'), may hold values from 0 to 4095, as said below
- edge_slot: int32 [393216], P('band'), may hold values from 0 to 895, as said below
- w_send: bfloat16 [512, 512], P(None, 'mp'), may hold values from -0.25 to 0.25
- w_recv: bfloat16 [512, 512], P(None, 'mp'), may hold values from -0.25 to 0.25
- w_edge: bfloat16 [512, 512], P(None, 'mp'), may hold values from -0.25 to 0.25
- edge_bias: float32 [512], P('mp'), may hold values from -3 to 3
- w_out: bfloat16 [512, 512], P('mp'), may hold values from -0.25 to 0.25
Outputs:
- grid_grad: bfloat16 [262144, 512], P('band', 'mp')
- node_grad: bfloat16 [40960, 512], P('band', 'mp')
Inputs may be any that keep to these rules, and one draw needn't show every extreme that they name: request[p, k, c] is a node of patch p, numbered within the patch, wanted by band p + 3 - k, or -1 for an empty slot; where that band lies outside 0 to 63 all slots are -1; otherwise the live slots come first, name distinct nodes and number 1 or more; request[p, 3, c] is live for every c. `edge_sender`: within a band the senders never fall, and each grid point of the band sends one or two edges. edge_slot = k * 128 + c, the patch b + k - 3 of the edge's band b lies in 0 to 63, and request[b + k - 3, k, c] is never -1.
All inputs are finite; a program needn't handle non-finite values.
Results may differ from a plain program's by a relative error of at most 0.015.
Values may be sent and summed in bfloat16 or wider, within the bound.
No kernel may reach another device: no remote copies, remote signals or barrier semaphores. Data moves between devices by JAX's collectives and lax.ppermute only.
A program may use at most 64 MiB of HBM per device.

v0:
```python
import jax
import jax.numpy as jnp
from jax import lax
from jax.experimental import pallas as pl
from jax.experimental.pallas import tpu as pltpu
from jax.sharding import PartitionSpec as P


F32 = jnp.float32
BF16 = jnp.bfloat16
I32 = jnp.int32
I16 = jnp.int16
LANES = 128
BLOCK = 256
WINDOW = 384
ROWS = 1024
OWN = 3
OTHERS = (2, 4, 1, 5, 0, 6)
ORDER = (OWN, *OTHERS)


def ring(shard, axis, by):
    devices = lax.axis_size(axis)
    return lax.ppermute(shard, axis, [(i, (i + by) % devices) for i in range(devices)])


def from_peers(shard, by_shift):
    return [ring(shard[s] if by_shift else shard, "mp", s) for s in (1, 2, 3)]


def dot(a, b):
    return jnp.dot(a, b, preferred_element_type=F32)


def dot_t(a, b):
    return lax.dot_general(a, b, (((1,), (1,)), ((), ())), preferred_element_type=F32)


def column(row):
    return jnp.transpose(jnp.broadcast_to(row, (LANES, row.shape[1])))


def one_hot(ids, width):
    short = ids.astype(I16)
    lane = lax.broadcasted_iota(I32, ids.shape, 1).astype(I16)
    one, zero = jnp.ones(ids.shape, BF16), jnp.zeros(ids.shape, BF16)
    return jnp.concatenate(
        [jnp.where(short == lane + jnp.int16(LANES * t), one, zero) for t in range(width // LANES)], axis=1
    )


def one_hot_t(row, height):
    shape = (height, row.shape[1])
    return (jnp.broadcast_to(row, shape) == lax.broadcasted_iota(I32, shape, 0)).astype(F32).astype(BF16)


def call(kernel, out_shape, args, flops, nbytes, mib, **kw):
    return pl.pallas_call(
        kernel,
        out_shape=out_shape,
        cost_estimate=pl.CostEstimate(flops=flops, bytes_accessed=nbytes, transcendentals=0),
        compiler_params=pltpu.CompilerParams(vmem_limit_bytes=mib * 2**20),
        **kw,
    )(*args)


def shape(dims, dtype):
    return jax.ShapeDtypeStruct(dims, dtype)


def pick_kernel(lat_ref, grad_ref, counts_ref, req_ref, *out_refs):
    nodes = lat_ref.shape[0]
    scaled = []
    for t in range(nodes // LANES):
        rows = pl.ds(LANES * t, LANES)
        count = column(counts_ref[t : t + 1, :]).astype(F32)
        scaled.append((grad_ref[rows, :].astype(F32) / count).astype(BF16))
    both = jnp.concatenate([lat_ref[...], jnp.concatenate(scaled, axis=0)], axis=1)
    for k, out_ref in enumerate(out_refs):
        ids = column(req_ref[k])
        out_ref[...] = dot(one_hot(ids, nodes), both).astype(BF16)


def join_kernel(*refs):
    out_ref = refs[-1]
    for n, ref in enumerate(refs[:-1]):
        out_ref[n * LANES : (n + 1) * LANES, :] = ref[...]


def pre_kernel(base_ref, lat_ref, edge_ref, send_ref, slot_ref, wsend_ref, wedge_ref, bias_ref, *refs):
    out_ref, slot_hot_ref, send_hot_ref, split_ref = refs
    cols = wsend_ref.shape[1]
    slot_count = slot_hot_ref.shape[1]
    lat_steps = lat_ref.shape[0] // ROWS
    steps = edge_ref.shape[0] // ROWS

    def at(step):
        return pl.ds(pl.multiple_of(step * ROWS, ROWS), ROWS)

    @pl.loop(0, lat_steps)
    def _(step):
        proj = dot(lat_ref[at(step), :], wsend_ref[...])
        upper = proj.astype(BF16)
        lower = (proj - upper.astype(F32)).astype(BF16)
        split_ref[at(step), :] = jnp.concatenate([upper, lower], axis=1)

    @pl.loop(0, steps)
    def _(step):
        for sub in range(ROWS // BLOCK):
            block = step * (ROWS // BLOCK) + sub
            rows = pl.ds(pl.multiple_of(block * BLOCK, BLOCK), BLOCK)
            base = pl.multiple_of(base_ref[block], LANES)
            send_row = send_ref[pl.ds(block, 1), :] - base
            slot_row = slot_ref[pl.ds(block, 1), :]
            send_hot = one_hot(column(send_row), WINDOW)
            picked = dot(send_hot, split_ref[pl.ds(base, WINDOW), :])
            value = picked[:, :cols] + picked[:, cols:] + dot(edge_ref[rows, :], wedge_ref[...])
            out_ref[rows, :] = value + bias_ref[...]
            send_hot_ref[rows, :] = send_hot
            slot_hot_ref[rows, :] = one_hot(column(slot_row), slot_count)


def main_kernel(base_ref, chan_ref, *refs):
    slots_in, recv_ref, wout_ref = refs[:4], refs[4], refs[5]
    pre_ref, slot_hot_ref, send_hot_ref = refs[6:9]
    sums, slots = refs[9:13], refs[13:20]
    table_ref, acc_ref, slot_acc_ref, grad_ref = refs[20:]
    cols = recv_ref.shape[1]
    steps = pre_ref.shape[0] // ROWS

    acc_ref[...] = jnp.zeros_like(acc_ref)
    slot_acc_ref[...] = jnp.zeros_like(slot_acc_ref)
    proj = back = None
    for s, ref in enumerate(slots_in):
        chan = pl.ds(pl.multiple_of(chan_ref[s], LANES), LANES)
        p = dot(ref[:, :LANES], recv_ref[chan, :])
        b = dot_t(ref[:, LANES:], wout_ref[:, chan])
        proj = p if proj is None else proj + p
        back = b if back is None else back + b
    both = jnp.concatenate([proj, back], axis=1).astype(BF16)
    for n, k in enumerate(ORDER):
        table_ref[k * LANES : (k + 1) * LANES, :] = both[n * LANES : (n + 1) * LANES, :]

    def at(start, size):
        return pl.ds(pl.multiple_of(start, size), size)

    def gradient(step):
        rows = at(step * ROWS, ROWS)
        got = dot(slot_hot_ref[rows, :], table_ref[...])
        pre = pre_ref[rows, :] + got[:, :cols]
        sig = jax.nn.sigmoid(pre)
        return jnp.transpose(got[:, cols:] * (sig * (1.0 + pre * (1.0 - sig)))).astype(BF16)

    def collect(step, grad):
        slot_acc_ref[...] += dot(grad, slot_hot_ref[at(step * ROWS, ROWS), :])
        for sub in range(ROWS // BLOCK):
            block = step * (ROWS // BLOCK) + sub
            base = pl.multiple_of(base_ref[block], LANES)
            part = grad[:, sub * BLOCK : (sub + 1) * BLOCK]
            acc_ref[:, pl.ds(base, WINDOW)] += dot(part, send_hot_ref[at(block * BLOCK, BLOCK), :])

    grad_ref[...] = gradient(0)

    @pl.loop(1, steps)
    def _(step):
        before = grad_ref[...]
        grad = gradient(step)
        collect(step - 1, before)
        grad_ref[...] = grad

    collect(steps - 1, grad_ref[...])
    quarter = sums[0].shape[0]
    for s, out_ref in enumerate(sums):
        first = pl.multiple_of(chan_ref[4 + s] // LANES * quarter, LANES)
        for n in range(quarter // LANES):
            part = acc_ref[:, pl.ds(pl.multiple_of(first + n * LANES, LANES), LANES)]
            out_ref[n * LANES : (n + 1) * LANES, :] = jnp.transpose(part).astype(BF16)
    for k, out_ref in enumerate(slots):
        out_ref[...] = jnp.transpose(slot_acc_ref[:, k * LANES : (k + 1) * LANES]).astype(BF16)


def back_kernel(chan_ref, *refs):
    parts, weights, outs = refs[:4], refs[4:8], refs[8:12]
    x = jnp.concatenate([r[...] for r in parts], axis=1)
    for s, out_ref in enumerate(outs):
        chan = pl.ds(pl.multiple_of(chan_ref[4 + s], LANES), LANES)
        w = jnp.concatenate([r[chan, :] for r in weights], axis=1)
        out_ref[...] = dot_t(x, w).astype(BF16)


def place_kernel(chan_ref, *refs):
    out_ref = refs[4]
    quarter = refs[0].shape[0]
    for s in range(4):
        first = pl.multiple_of(chan_ref[s] // LANES * quarter, LANES)
        out_ref[pl.ds(first, quarter), :] = refs[s][...]


def node_kernel(chan_ref, req_ref, recv_ref, *refs):
    returned, outs = refs[:7], refs[7:11]
    nodes = outs[0].shape[0]
    picks = jnp.concatenate([one_hot_t(req_ref[k], nodes) for k in range(len(returned))], axis=1)
    total = dot(picks, jnp.concatenate([ref[...] for ref in returned], axis=0))
    upper = total.astype(BF16)
    lower = (total - upper.astype(F32)).astype(BF16)
    for s, out_ref in enumerate(outs):
        w = recv_ref[pl.ds(pl.multiple_of(chan_ref[4 + s], LANES), LANES), :]
        out_ref[...] = (dot_t(upper, w) + dot_t(lower, w)).astype(out_ref.dtype)


def per_device(
    grid_latent,
    edge_latent,
    mesh_latent,
    mesh_grad,
    counts,
    request,
    edge_sender,
    edge_slot,
    w_send,
    w_recv,
    w_edge,
    edge_bias,
    w_out,
):
    span, capacity = request.shape[1:]
    nodes = mesh_latent.shape[0]
    grid_rows, latent = grid_latent.shape
    edges = edge_latent.shape[0]
    cols = w_send.shape[1]
    slot_count = span * capacity
    blocks = edges // BLOCK
    quarter = grid_rows // 4
    mine = lax.axis_index("mp")
    turns = jnp.arange(4, dtype=I32)
    chan = jnp.concatenate([(mine - turns) % 4, (mine + turns) % 4]).astype(I32) * LANES
    senders = edge_sender.reshape(blocks, BLOCK)
    slot_ids = edge_slot.reshape(blocks, BLOCK)
    base = jnp.minimum(senders[:, 0] // LANES * LANES, grid_rows - WINDOW)
    wanted = request.reshape(span, 1, capacity)

    smem = pl.BlockSpec(memory_space=pltpu.SMEM)
    vmem = pl.BlockSpec(memory_space=pltpu.VMEM)
    picked = call(
        pick_kernel,
        [shape((capacity, 2 * LANES), BF16)] * span,
        (mesh_latent, mesh_grad, counts.reshape(nodes // LANES, LANES), wanted),
        2 * slot_count * nodes * 2 * LANES,
        2 * (2 * nodes + 2 * slot_count) * LANES,
        60,
        in_specs=[vmem] * 4,
        out_specs=[vmem] * span,
    )
    slots_here = call(
        join_kernel,
        shape((slot_count, 2 * LANES), BF16),
        (picked[OWN], *[ring(picked[k], "band", OWN - k) for k in OTHERS]),
        0,
        8 * slot_count * LANES,
        4,
        in_specs=[vmem] * span,
        out_specs=vmem,
    )
    slots_all = [slots_here] + from_peers(slots_here, False)
    send_peers = from_peers(w_send, False)

    pre, *hots = call(
        pre_kernel,
        [shape((edges, cols), F32), shape((edges, slot_count), BF16), shape((edges, WINDOW), BF16)],
        (base, grid_latent, edge_latent, senders, slot_ids, w_send, w_edge, edge_bias.reshape(1, cols)),
        2 * edges * cols * (latent + 2 * WINDOW) + 2 * grid_rows * latent * cols,
        2 * (edges + grid_rows) * latent + 4 * edges * cols,
        6,
        in_specs=[smem] + [vmem] * 7,
        out_specs=[vmem] * 3,
        scratch_shapes=[pltpu.VMEM((grid_rows, 2 * cols), BF16)],
    )
    result = call(
        main_kernel,
        [shape((quarter, cols), BF16)] * 4 + [shape((capacity, cols), BF16)] * span,
        (base, chan, *slots_all, w_recv, w_out, pre, *hots),
        2 * edges * cols * (3 * slot_count + WINDOW),
        4 * edges * cols,
        8,
        in_specs=[smem, smem] + [vmem] * 9,
        out_specs=[vmem] * 11,
        scratch_shapes=[
            pltpu.VMEM((slot_count, 2 * cols), BF16),
            pltpu.VMEM((cols, grid_rows), F32),
            pltpu.VMEM((cols, slot_count), F32),
            pltpu.VMEM((cols, ROWS), BF16),
        ],
    )
    sums, slot_sums = result[:4], result[4:]

    back = {k: ring(slot_sums[k], "band", k - OWN) for k in OTHERS}
    back[OWN] = slot_sums[OWN]
    hidden_parts = [sums[0]] + from_peers(sums, True)
    node_terms = call(
        node_kernel,
        [shape((nodes, LANES), F32)] + [shape((nodes, LANES), BF16)] * 3,
        (chan, wanted, w_recv, *[back[k] for k in range(span)]),
        2 * nodes * cols * (slot_count + 2 * latent),
        2 * nodes * latent,
        8,
        in_specs=[smem] + [vmem] * 9,
        out_specs=[vmem] * 4,
    )
    terms = call(
        back_kernel,
        [shape((quarter, LANES), BF16)] * 4,
        (chan, *hidden_parts, w_send, *send_peers),
        2 * quarter * latent * 4 * cols,
        2 * quarter * latent * 2,
        8,
        in_specs=[smem] + [vmem] * 8,
        out_specs=[vmem] * 4,
    )
    row_parts = [terms[0]] + from_peers(terms, True)
    grid_grad = call(
        place_kernel,
        shape((grid_rows, LANES), BF16),
        (chan, *row_parts),
        0,
        4 * grid_rows * LANES,
        8,
        in_specs=[smem] + [vmem] * 4,
        out_specs=vmem,
    )
    node_grad = node_terms[0]
    for part in from_peers(node_terms, True):
        node_grad = node_grad + part.astype(F32)
    return (grid_grad, node_grad.astype(BF16))


def solution(mesh):
    in_specs = (
        P("band", None),
        P("band", None),
        P("band", "mp"),
        P("band", "mp"),
        P("band"),
        P("band", None, None),
        P("band"),
        P("band"),
        P(None, "mp"),
        P(None, "mp"),
        P(None, "mp"),
        P("mp"),
        P("mp", None),
    )
    out_specs = (P("band", "mp"), P("band", "mp"))

    return jax.shard_map(per_device, mesh=mesh, in_specs=in_specs, out_specs=out_specs, check_vma=False)
```

profile of v0, /device:TPU:1, one launch (start us, length us, event | category | flops | bytes accessed | tf_op | source)
XLA Modules:
  0.0 106.2 jit_solution(14218322760540991126)
XLA Ops:
  0.6 2.3 %shard_map.140 = (bf16[128,256]{1,0:T(8,128)(2,1)}, bf16[128,256]{1,0:T(8,128)(2,1)}, bf16[128,256]{1,0:T(8,128)(2,1)}, bf16[128,256]{1,0:T(8,128)(2,1)}, bf16[1...) custom-call(bf16[640,128]{1,0:T(8,128)(2,1)} %lat_ref.2, bf16[640,128]{1,0:T(8,128)(2,1)} %grad_ref.1, ...), custom_call_target="tpu_custom_call" | custom-call | flops 293601280 | bytes 786432 | tf_op jit(solution)/shard_map/pallas_call | solution.py:58
  2.9 3.0 %collective-permute-start = (bf16[128,256]{1,0:T(8,128)(2,1)}, bf16[128,256]{1,0:T(8,128)(2,1)S(1)}, u32[]{:S(2)}, u32[]{:S(2)}) collective-permute-start(bf16[128,256]{1,0:T(8,128)(2,1)} %get-tuple-element.32), channel_id=1, source_target_pairs={{0,4},{4,8},{8,12},{12,16},{16,20},{20,24},{24,28},{28,32},{32,36}... | collective-permute-start | bytes 196616 | tf_op jit(solution)/shard_map/ppermute | solution.py:24
  5.9 0.2 collective-permute-start.1
  6.1 1.4 %collective-permute-start.2 = (bf16[128,256]{1,0:T(8,128)(2,1)}, bf16[128,256]{1,0:T(8,128)(2,1)S(1)}, u32[]{:S(2)}, u32[]{:S(2)}) collective-permute-start(bf16[128,256]{1,0:T(8,128)(2,1)} %get-tuple-element.34), channel_id=1, source_target_pairs={{0,8},{4,12},{8,16},{12,20},{16,24},{20,28},{24,32},{28,36},{32,40... | collective-permute-start | bytes 196616 | tf_op jit(solution)/shard_map/ppermute | solution.py:24
  7.6 4.9 %collective-permute-start.3 = (bf16[128,256]{1,0:T(8,128)(2,1)}, bf16[128,256]{1,0:T(8,128)(2,1)S(1)}, u32[]{:S(2)}, u32[]{:S(2)}) collective-permute-start(bf16[128,256]{1,0:T(8,128)(2,1)} %get-tuple-element.35), channel_id=1, source_target_pairs={{0,248},{4,252},{8,0},{12,4},{16,8},{20,12},{24,16},{28,20},{32,24... | collective-permute-start | bytes 196616 | tf_op jit(solution)/shard_map/ppermute | solution.py:24
  12.4 0.7 reshape.19.send_ref
  13.3 0.7 reshape.22.slot_ref
  14.1 5.1 %collective-permute-start.5 = (bf16[128,256]{1,0:T(8,128)(2,1)}, bf16[128,256]{1,0:T(8,128)(2,1)S(1)}, u32[]{:S(2)}, u32[]{:S(2)}) collective-permute-start(bf16[128,256]{1,0:T(8,128)(2,1)} %get-tuple-element.37), channel_id=1, source_target_pairs={{0,244},{4,248},{8,252},{12,0},{16,4},{20,8},{24,12},{28,16},{32,2... | collective-permute-start | bytes 196616 | tf_op jit(solution)/shard_map/ppermute | solution.py:24
  19.3 1.2 %collective-permute-start.12 = (bf16[512,128]{1,0:T(8,128)(2,1)}, bf16[512,128]{1,0:T(8,128)(2,1)S(1)}, u32[]{:S(2)}, u32[]{:S(2)}) collective-permute-start(bf16[512,128]{1,0:T(8,128)(2,1)} %refs_4_.3), channel_id=1, source_target_pairs={{0,1},{1,2},{2,3},{3,0},{4,5},{5,6},{6,7},{7,4},{8,9},{9,10},{10,1... | collective-permute-start | bytes 393224 | tf_op jit(solution)/shard_map/ppermute | solution.py:24
  20.5 0.3 collective-permute-done.5.refs_6_
  20.9 0.8 copy-done.6
  21.7 1.3 %collective-permute-start.6 = (bf16[896,256]{1,0:T(8,128)(2,1)S(1)}, bf16[896,256]{1,0:T(8,128)(2,1)S(1)}, u32[]{:S(2)}, u32[]{:S(2)}) collective-permute-start(bf16[896,256]{1,0:T(8,128)(2,1)S(1)} %shard_map.141.refs_0_), channel_id=1, source_target_pairs={{0,1},{1,2},{2,3},{3,0},{4,5},{5,6},{6,7},{7,4},{8,9},{9,10},{10,1... | collective-permute-start | bytes 1376264 | tf_op jit(solution)/shard_map/ppermute | solution.py:24
  23.0 2.4 %collective-permute-start.7 = (bf16[896,256]{1,0:T(8,128)(2,1)S(1)}, bf16[896,256]{1,0:T(8,128)(2,1)S(1)}, u32[]{:S(2)}, u32[]{:S(2)}) collective-permute-start(bf16[896,256]{1,0:T(8,128)(2,1)S(1)} %shard_map.141.refs_0_), channel_id=1, source_target_pairs={{0,2},{1,3},{2,0},{3,1},{4,6},{5,7},{6,4},{7,5},{8,10},{9,11},{10,... | collective-permute-start | bytes 1376264 | tf_op jit(solution)/shard_map/ppermute | solution.py:24
  25.5 1.2 %collective-permute-start.8 = (bf16[896,256]{1,0:T(8,128)(2,1)S(1)}, bf16[896,256]{1,0:T(8,128)(2,1)S(1)}, u32[]{:S(2)}, u32[]{:S(2)}) collective-permute-start(bf16[896,256]{1,0:T(8,128)(2,1)S(1)} %shard_map.141.refs_0_), channel_id=1, source_target_pairs={{0,3},{1,0},{2,1},{3,2},{4,7},{5,4},{6,5},{7,6},{8,11},{9,8},{10,9... | collective-permute-start | bytes 1376264 | tf_op jit(solution)/shard_map/ppermute | solution.py:24
  26.6 2.8 %copy-done = bf16[6144,512]{1,0:T(8,128)(2,1)S(1)} copy-done((bf16[6144,512]{1,0:T(8,128)(2,1)S(1)}, bf16[6144,512]{1,0:T(8,128)(2,1)}, u32[]{:S(2)}) %copy-start) | copy-done | bytes 6291480
  29.4 2.2 %copy-done.1 = bf16[4096,512]{1,0:T(8,128)(2,1)S(1)} copy-done((bf16[4096,512]{1,0:T(8,128)(2,1)S(1)}, bf16[4096,512]{1,0:T(8,128)(2,1)}, u32[]{:S(2)}) %copy-start.1) | copy-done | bytes 4194328
  31.6 0.9 copy-done.2
  32.5 0.9 copy-done.5
  33.4 0.7 copy-done.7
  34.1 7.1 %shard_map.142 = (f32[6144,128]{1,0:T(8,128)S(1)}, bf16[6144,896]{1,0:T(8,128)(2,1)S(1)}, bf16[6144,384]{1,0:T(8,128)(2,1)S(1)}) custom-call(s32[24]{0:T(128)S(1)} %multiply_minimum_fusion.base_ref, bf16[4096,512]{1,0:T(8,128)(2,1)S(1)} %copy-done.1, bf16[6144,512]{1,0:T(8,128)(2,1)S(1)} %copy-done, s32[24,256]{1,0:T(8,128)S(1)} %reshape.19.send_ref, ...), custom_call_target="tpu_custom_call" | custom-call | flops 2550136832 | bytes 13631488 | tf_op jit(solution)/shard_map/pallas_call | solution.py:58
  41.2 0.6 collective-permute-done.7.refs_2_
  41.9 9.4 %shard_map.143 = (bf16[1024,128]{1,0:T(8,128)(2,1)S(1)}, bf16[1024,128]{1,0:T(8,128)(2,1)S(1)}, bf16[1024,128]{1,0:T(8,128)(2,1)S(1)}, bf16[1024,128]{1,0:T(8,12...) custom-call(s32[24]{0:T(128)S(1)} %multiply_minimum_fusion.base_ref,, ...), custom_call_target="tpu_custom_call" | custom-call | flops 4831838208 | bytes 3145728 | tf_op jit(solution)/shard_map/pallas_call | solution.py:58
  51.4 2.6 %collective-permute-start.10 = (bf16[1024,128]{1,0:T(8,128)(2,1)S(1)}, bf16[1024,128]{1,0:T(8,128)(2,1)S(1)}, u32[]{:S(2)}, u32[]{:S(2)}) collective-permute-start(bf16[1024,128]{1,0:T(8,128)(2,1)S(1)} %get-tuple-element.43), channel_id=1, source_target_pairs={{0,2},{1,3},{2,0},{3,1},{4,6},{5,7},{6,4},{7,5},{8,10},{9,11},{10,... | collective-permute-start | bytes 786440 | tf_op jit(solution)/shard_map/ppermute | solution.py:24
  53.9 10.5 %collective-permute-start.18 = (bf16[128,128]{1,0:T(8,128)(2,1)S(1)}, bf16[128,128]{1,0:T(8,128)(2,1)S(1)}, u32[]{:S(2)}, u32[]{:S(2)}) collective-permute-start(bf16[128,128]{1,0:T(8,128)(2,1)S(1)} %get-tuple-element.49), channel_id=1, source_target_pairs={{0,244},{4,248},{8,252},{12,0},{16,4},{20,8},{24,12},{28,16},{32,2... | collective-permute-start | bytes 98312 | tf_op jit(solution)/shard_map/ppermute | solution.py:24
  64.4 0.4 collective-permute-start.20
  64.8 1.4 %collective-permute-start.21 = (bf16[128,128]{1,0:T(8,128)(2,1)S(1)}, bf16[128,128]{1,0:T(8,128)(2,1)S(1)}, u32[]{:S(2)}, u32[]{:S(2)}) collective-permute-start(bf16[128,128]{1,0:T(8,128)(2,1)S(1)} %get-tuple-element.53), channel_id=1, source_target_pairs={{0,4},{4,8},{8,12},{12,16},{16,20},{20,24},{24,28},{28,32},{32,36}... | collective-permute-start | bytes 98312 | tf_op jit(solution)/shard_map/ppermute | solution.py:24
  66.2 1.5 %collective-permute-start.22 = (bf16[128,128]{1,0:T(8,128)(2,1)S(1)}, bf16[128,128]{1,0:T(8,128)(2,1)S(1)}, u32[]{:S(2)}, u32[]{:S(2)}) collective-permute-start(bf16[128,128]{1,0:T(8,128)(2,1)S(1)} %get-tuple-element.54), channel_id=1, source_target_pairs={{0,8},{4,12},{8,16},{12,20},{16,24},{20,28},{24,32},{28,36},{32,40... | collective-permute-start | bytes 98312 | tf_op jit(solution)/shard_map/ppermute | solution.py:24
  67.7 1.3 %collective-permute-start.23 = (bf16[128,128]{1,0:T(8,128)(2,1)S(1)}, bf16[128,128]{1,0:T(8,128)(2,1)S(1)}, u32[]{:S(2)}, u32[]{:S(2)}) collective-permute-start(bf16[128,128]{1,0:T(8,128)(2,1)S(1)} %get-tuple-element.55), channel_id=1, source_target_pairs={{0,12},{4,16},{8,20},{12,24},{16,28},{20,32},{24,36},{28,40},{32,4... | collective-permute-start | bytes 98312 | tf_op jit(solution)/shard_map/ppermute | solution.py:24
  69.0 1.3 %collective-permute-start.11 = (bf16[1024,128]{1,0:T(8,128)(2,1)S(1)}, bf16[1024,128]{1,0:T(8,128)(2,1)S(1)}, u32[]{:S(2)}, u32[]{:S(2)}) collective-permute-start(bf16[1024,128]{1,0:T(8,128)(2,1)S(1)} %get-tuple-element.44), channel_id=1, source_target_pairs={{0,3},{1,0},{2,1},{3,2},{4,7},{5,4},{6,5},{7,6},{8,11},{9,8},{10,9... | collective-permute-start | bytes 786440 | tf_op jit(solution)/shard_map/ppermute | solution.py:24
  70.3 0.1 collective-permute-start.9
  70.4 2.9 %collective-permute-done.22.refs_5_ = bf16[128,128]{1,0:T(8,128)(2,1)S(1)} collective-permute-done((bf16[128,128]{1,0:T(8,128)(2,1)S(1)}, bf16[128,128]{1,0:T(8,128)(2,1)S(1)}, u32[]{:S(2)}, u32[]{:S(2)}) %collective-permute-start.22) | collective-permute-done | bytes 32800 | tf_op jit(solution)/shard_map/ppermute | solution.py:24
  73.4 0.6 collective-permute-start.13
  74.0 0.4 collective-permute-done.23.refs_6_
  74.3 2.2 %collective-permute-start.14 = (bf16[512,128]{1,0:T(8,128)(2,1)S(1)}, bf16[512,128]{1,0:T(8,128)(2,1)S(1)}, u32[]{:S(2)}, u32[]{:S(2)}) collective-permute-start(bf16[512,128]{1,0:T(8,128)(2,1)S(1)} %copy-done.5), channel_id=1, source_target_pairs={{0,3},{1,0},{2,1},{3,2},{4,7},{5,4},{6,5},{7,6},{8,11},{9,8},{10,9... | collective-permute-start | bytes 393224 | tf_op jit(solution)/shard_map/ppermute | solution.py:24
  76.5 1.8 %shard_map.146 = (f32[640,128]{1,0:T(8,128)S(1)}, bf16[640,128]{1,0:T(8,128)(2,1)S(1)}, bf16[640,128]{1,0:T(8,128)(2,1)S(1)}, bf16[640,128]{1,0:T(8,128)(2,1)S(1)}) custom-call(s32[8]{0:T(128)S(1)} %add_multiply_fusion.chan_ref, s32[7,1,128]{2,1,0:T(1,128)S(1)} %bitcast.5, bf16[512,128]{1,0:T(8,128)(2,1)S(1)} %copy-done.4, ...), custom_call_target="tpu_custom_call" | custom-call | flops 314572800 | bytes 655360 | tf_op jit(solution)/shard_map/pallas_call | solution.py:58
  78.3 2.0 %collective-permute-done.13.refs_6_ = bf16[512,128]{1,0:T(8,128)(2,1)S(1)} collective-permute-done((bf16[512,128]{1,0:T(8,128)(2,1)S(1)}, bf16[512,128]{1,0:T(8,128)(2,1)S(1)}, u32[]{:S(2)}, u32[]{:S(2)}) %collective-permute-start.13) | collective-permute-done | bytes 131104 | tf_op jit(solution)/shard_map/ppermute | solution.py:24
  80.4 2.0 %collective-permute-done.14.refs_7_ = bf16[512,128]{1,0:T(8,128)(2,1)S(1)} collective-permute-done((bf16[512,128]{1,0:T(8,128)(2,1)S(1)}, bf16[512,128]{1,0:T(8,128)(2,1)S(1)}, u32[]{:S(2)}, u32[]{:S(2)}) %collective-permute-start.14) | collective-permute-done | bytes 131104 | tf_op jit(solution)/shard_map/ppermute | solution.py:24
  82.4 1.4 %collective-permute-start.25 = (bf16[640,128]{1,0:T(8,128)(2,1)S(1)}, bf16[640,128]{1,0:T(8,128)(2,1)S(1)}, u32[]{:S(2)}, u32[]{:S(2)}) collective-permute-start(bf16[640,128]{1,0:T(8,128)(2,1)S(1)} %get-tuple-element.58), channel_id=1, source_target_pairs={{0,2},{1,3},{2,0},{3,1},{4,6},{5,7},{6,4},{7,5},{8,10},{9,11},{10,... | collective-permute-start | bytes 491528 | tf_op jit(solution)/shard_map/ppermute | solution.py:24
  83.8 2.5 %collective-permute-start.26 = (bf16[640,128]{1,0:T(8,128)(2,1)S(1)}, bf16[640,128]{1,0:T(8,128)(2,1)S(1)}, u32[]{:S(2)}, u32[]{:S(2)}) collective-permute-start(bf16[640,128]{1,0:T(8,128)(2,1)S(1)} %get-tuple-element.59), channel_id=1, source_target_pairs={{0,3},{1,0},{2,1},{3,2},{4,7},{5,4},{6,5},{7,6},{8,11},{9,8},{10,9... | collective-permute-start | bytes 491528 | tf_op jit(solution)/shard_map/ppermute | solution.py:24
  86.3 1.8 %shard_map.144 = (bf16[1024,128]{1,0:T(8,128)(2,1)S(1)}, bf16[1024,128]{1,0:T(8,128)(2,1)S(1)}, bf16[1024,128]{1,0:T(8,128)(2,1)S(1)}, bf16[1024,128]{1,0:T(8,128)(2,1)S(1)}) custom-call(s32[8]{0:T(128)S(1)} %add_multiply_fusion.chan_ref, bf16[1024,128]{1,0:T(8,128)(2,1)S(1)} %get-tuple-element.41.refs_0_, ...), custom_call_target="tpu_custom_call" | custom-call | flops 536870912 | bytes 2097152 | tf_op jit(solution)/shard_map/pallas_call | solution.py:58
  88.2 1.5 %collective-permute-start.16 = (bf16[1024,128]{1,0:T(8,128)(2,1)S(1)}, bf16[1024,128]{1,0:T(8,128)(2,1)S(1)}, u32[]{:S(2)}, u32[]{:S(2)}) collective-permute-start(bf16[1024,128]{1,0:T(8,128)(2,1)S(1)} %get-tuple-element.47), channel_id=1, source_target_pairs={{0,2},{1,3},{2,0},{3,1},{4,6},{5,7},{6,4},{7,5},{8,10},{9,11},{10,... | collective-permute-start | bytes 786440 | tf_op jit(solution)/shard_map/ppermute | solution.py:24
  89.7 2.0 %collective-permute-start.17 = (bf16[1024,128]{1,0:T(8,128)(2,1)S(1)}, bf16[1024,128]{1,0:T(8,128)(2,1)S(1)}, u32[]{:S(2)}, u32[]{:S(2)}) collective-permute-start(bf16[1024,128]{1,0:T(8,128)(2,1)S(1)} %get-tuple-element.48), channel_id=1, source_target_pairs={{0,3},{1,0},{2,1},{3,2},{4,7},{5,4},{6,5},{7,6},{8,11},{9,8},{10,9... | collective-permute-start | bytes 786440 | tf_op jit(solution)/shard_map/ppermute | solution.py:24
  91.7 1.7 %collective-permute-done.26 = bf16[640,128]{1,0:T(8,128)(2,1)S(1)} collective-permute-done((bf16[640,128]{1,0:T(8,128)(2,1)S(1)}, bf16[640,128]{1,0:T(8,128)(2,1)S(1)}, u32[]{:S(2)}, u32[]{:S(2)}) %collective-permute-start.26) | collective-permute-done | bytes 163872 | tf_op jit(solution)/shard_map/ppermute | solution.py:24
  93.4 0.7 add_convert_fusion
  94.1 2.6 %collective-permute-done.15.refs_1_ = bf16[1024,128]{1,0:T(8,128)(2,1)S(1)} collective-permute-done((bf16[1024,128]{1,0:T(8,128)(2,1)S(1)}, bf16[1024,128]{1,0:T(8,128)(2,1)S(1)}, u32[]{:S(2)}, u32[]{:S(2)}) %collective-permute-start.15) | collective-permute-done | bytes 262176 | tf_op jit(solution)/shard_map/ppermute | solution.py:24
  96.7 5.4 %collective-permute-done.16.refs_2_ = bf16[1024,128]{1,0:T(8,128)(2,1)S(1)} collective-permute-done((bf16[1024,128]{1,0:T(8,128)(2,1)S(1)}, bf16[1024,128]{1,0:T(8,128)(2,1)S(1)}, u32[]{:S(2)}, u32[]{:S(2)}) %collective-permute-start.16) | collective-permute-done | bytes 262176 | tf_op jit(solution)/shard_map/ppermute | solution.py:24
  102.1 2.4 %collective-permute-done.17.refs_3_ = bf16[1024,128]{1,0:T(8,128)(2,1)S(1)} collective-permute-done((bf16[1024,128]{1,0:T(8,128)(2,1)S(1)}, bf16[1024,128]{1,0:T(8,128)(2,1)S(1)}, u32[]{:S(2)}, u32[]{:S(2)}) %collective-permute-start.17) | collective-permute-done | bytes 262176 | tf_op jit(solution)/shard_map/ppermute | solution.py:24
  104.6 1.6 %shard_map.145 = bf16[4096,128]{1,0:T(8,128)(2,1)} custom-call(s32[8]{0:T(128)S(1)} %add_multiply_fusion.chan_ref, bf16[1024,128]{1,0:T(8,128)(2,1)S(1)} %get-tuple-element.45.refs_0_, bf16[1024,128]{1,0:T(8,128)(2,1)S(1)} %collective-permute-done.15.refs_1_, bf16[1024,128]{1,0:T(8,128)(2,1)S(1)} %collective-permute-done.16.refs_2_, ...), custom_call_target="tpu_custom_call" | custom-call | bytes 2097152 | tf_op jit(solution)/shard_map/pallas_call | solution.py:58
  (38 shorter events, 0.4 us)
Async XLA Ops:
  2.9 11.2 %collective-permute-start = (bf16[128,256]{1,0:T(8,128)(2,1)}, bf16[128,256]{1,0:T(8,128)(2,1)S(1)}, u32[]{:S(2)}, u32[]{:S(2)}) collective-permute-start(bf16[128,256]{1,0:T(8,128)(2,1)} %get-tuple-element.32), channel_id=1, source_target_pairs={{0,4},{4,8},{8,12},{12,16},{16,20},{20,24},{24,28},{28,32},{32,36}... | collective-permute-start | bytes 196616 | tf_op jit(solution)/shard_map/ppermute | solution.py:24
  5.9 13.4 %collective-permute-start.1 = (bf16[128,256]{1,0:T(8,128)(2,1)}, bf16[128,256]{1,0:T(8,128)(2,1)S(1)}, u32[]{:S(2)}, u32[]{:S(2)}) collective-permute-start(bf16[128,256]{1,0:T(8,128)(2,1)} %get-tuple-element.33), channel_id=1, source_target_pairs={{0,252},{4,0},{8,4},{12,8},{16,12},{20,16},{24,20},{28,24},{32,28}... | collective-permute-start | bytes 196616 | tf_op jit(solution)/shard_map/ppermute | solution.py:24
  6.1 14.4 %collective-permute-start.2 = (bf16[128,256]{1,0:T(8,128)(2,1)}, bf16[128,256]{1,0:T(8,128)(2,1)S(1)}, u32[]{:S(2)}, u32[]{:S(2)}) collective-permute-start(bf16[128,256]{1,0:T(8,128)(2,1)} %get-tuple-element.34), channel_id=1, source_target_pairs={{0,8},{4,12},{8,16},{12,20},{16,24},{20,28},{24,32},{28,36},{32,40... | collective-permute-start | bytes 196616 | tf_op jit(solution)/shard_map/ppermute | solution.py:24
  7.6 13.0 %collective-permute-start.3 = (bf16[128,256]{1,0:T(8,128)(2,1)}, bf16[128,256]{1,0:T(8,128)(2,1)S(1)}, u32[]{:S(2)}, u32[]{:S(2)}) collective-permute-start(bf16[128,256]{1,0:T(8,128)(2,1)} %get-tuple-element.35), channel_id=1, source_target_pairs={{0,248},{4,252},{8,0},{12,4},{16,8},{20,12},{24,16},{28,20},{32,24... | collective-permute-start | bytes 196616 | tf_op jit(solution)/shard_map/ppermute | solution.py:24
  12.4 8.1 %collective-permute-start.4 = (bf16[128,256]{1,0:T(8,128)(2,1)}, bf16[128,256]{1,0:T(8,128)(2,1)S(1)}, u32[]{:S(2)}, u32[]{:S(2)}) collective-permute-start(bf16[128,256]{1,0:T(8,128)(2,1)} %get-tuple-element.36), channel_id=1, source_target_pairs={{0,12},{4,16},{8,20},{12,24},{16,28},{20,32},{24,36},{28,40},{32,4... | collective-permute-start | bytes 196616 | tf_op jit(solution)/shard_map/ppermute | solution.py:24
  14.1 6.8 %collective-permute-start.5 = (bf16[128,256]{1,0:T(8,128)(2,1)}, bf16[128,256]{1,0:T(8,128)(2,1)S(1)}, u32[]{:S(2)}, u32[]{:S(2)}) collective-permute-start(bf16[128,256]{1,0:T(8,128)(2,1)} %get-tuple-element.37), channel_id=1, source_target_pairs={{0,244},{4,248},{8,252},{12,0},{16,4},{20,8},{24,12},{28,16},{32,2... | collective-permute-start | bytes 196616 | tf_op jit(solution)/shard_map/ppermute | solution.py:24
  19.3 45.6 %collective-permute-start.12 = (bf16[512,128]{1,0:T(8,128)(2,1)}, bf16[512,128]{1,0:T(8,128)(2,1)S(1)}, u32[]{:S(2)}, u32[]{:S(2)}) collective-permute-start(bf16[512,128]{1,0:T(8,128)(2,1)} %refs_4_.3), channel_id=1, source_target_pairs={{0,1},{1,2},{2,3},{3,0},{4,5},{5,6},{6,7},{7,4},{8,9},{9,10},{10,1... | collective-permute-start | bytes 393224 | tf_op jit(solution)/shard_map/ppermute | solution.py:24
  20.9 0.8 copy-start.6
  21.7 19.5 %collective-permute-start.6 = (bf16[896,256]{1,0:T(8,128)(2,1)S(1)}, bf16[896,256]{1,0:T(8,128)(2,1)S(1)}, u32[]{:S(2)}, u32[]{:S(2)}) collective-permute-start(bf16[896,256]{1,0:T(8,128)(2,1)S(1)} %shard_map.141.refs_0_), channel_id=1, source_target_pairs={{0,1},{1,2},{2,3},{3,0},{4,5},{5,6},{6,7},{7,4},{8,9},{9,10},{10,1... | collective-permute-start | bytes 1376264 | tf_op jit(solution)/shard_map/ppermute | solution.py:24
  23.0 18.9 %collective-permute-start.7 = (bf16[896,256]{1,0:T(8,128)(2,1)S(1)}, bf16[896,256]{1,0:T(8,128)(2,1)S(1)}, u32[]{:S(2)}, u32[]{:S(2)}) collective-permute-start(bf16[896,256]{1,0:T(8,128)(2,1)S(1)} %shard_map.141.refs_0_), channel_id=1, source_target_pairs={{0,2},{1,3},{2,0},{3,1},{4,6},{5,7},{6,4},{7,5},{8,10},{9,11},{10,... | collective-permute-start | bytes 1376264 | tf_op jit(solution)/shard_map/ppermute | solution.py:24
  25.5 16.4 %collective-permute-start.8 = (bf16[896,256]{1,0:T(8,128)(2,1)S(1)}, bf16[896,256]{1,0:T(8,128)(2,1)S(1)}, u32[]{:S(2)}, u32[]{:S(2)}) collective-permute-start(bf16[896,256]{1,0:T(8,128)(2,1)S(1)} %shard_map.141.refs_0_), channel_id=1, source_target_pairs={{0,3},{1,0},{2,1},{3,2},{4,7},{5,4},{6,5},{7,6},{8,11},{9,8},{10,9... | collective-permute-start | bytes 1376264 | tf_op jit(solution)/shard_map/ppermute | solution.py:24
  26.6 2.8 %copy-start = (bf16[6144,512]{1,0:T(8,128)(2,1)S(1)}, bf16[6144,512]{1,0:T(8,128)(2,1)}, u32[]{:S(2)}) copy-start(bf16[6144,512]{1,0:T(8,128)(2,1)} %edge_ref.1) | copy-start | bytes 18874372
  29.4 2.2 %copy-start.1 = (bf16[4096,512]{1,0:T(8,128)(2,1)S(1)}, bf16[4096,512]{1,0:T(8,128)(2,1)}, u32[]{:S(2)}) copy-start(bf16[4096,512]{1,0:T(8,128)(2,1)} %lat_ref.3) | copy-start | bytes 12582916
  31.6 0.9 copy-start.2
  32.5 0.9 copy-start.5
  33.4 0.7 copy-start.7
  34.1 7.8 %copy-start.3 = (bf16[128,512]{1,0:T(8,128)(2,1)S(1)}, bf16[128,512]{1,0:T(8,128)(2,1)}, u32[]{:S(2)}) copy-start(bf16[128,512]{1,0:T(8,128)(2,1)} %refs_5_.1) | copy-start | bytes 393220
  34.1 7.8 %copy-start.4 = (bf16[512,128]{1,0:T(8,128)(2,1)S(1)}, bf16[512,128]{1,0:T(8,128)(2,1)}, u32[]{:S(2)}) copy-start(bf16[512,128]{1,0:T(8,128)(2,1)} %recv_ref.1) | copy-start | bytes 393220
  41.9 34.6 %copy-start.8 = (s32[1,7,128]{2,0,1:T(1,128)S(1)}, s32[1,7,128]{2,0,1:T(1,128)}, u32[]{:S(2)}) copy-start(s32[1,7,128]{2,0,1:T(1,128)} %param.18) | copy-start | bytes 10756
  51.4 32.4 %collective-permute-start.10 = (bf16[1024,128]{1,0:T(8,128)(2,1)S(1)}, bf16[1024,128]{1,0:T(8,128)(2,1)S(1)}, u32[]{:S(2)}, u32[]{:S(2)}) collective-permute-start(bf16[1024,128]{1,0:T(8,128)(2,1)S(1)} %get-tuple-element.43), channel_id=1, source_target_pairs={{0,2},{1,3},{2,0},{3,1},{4,6},{5,7},{6,4},{7,5},{8,10},{9,11},{10,... | collective-permute-start | bytes 786440 | tf_op jit(solution)/shard_map/ppermute | solution.py:24
  53.9 12.3 %collective-permute-start.18 = (bf16[128,128]{1,0:T(8,128)(2,1)S(1)}, bf16[128,128]{1,0:T(8,128)(2,1)S(1)}, u32[]{:S(2)}, u32[]{:S(2)}) collective-permute-start(bf16[128,128]{1,0:T(8,128)(2,1)S(1)} %get-tuple-element.49), channel_id=1, source_target_pairs={{0,244},{4,248},{8,252},{12,0},{16,4},{20,8},{24,12},{28,16},{32,2... | collective-permute-start | bytes 98312 | tf_op jit(solution)/shard_map/ppermute | solution.py:24
  64.4 3.2 %collective-permute-start.19 = (bf16[128,128]{1,0:T(8,128)(2,1)S(1)}, bf16[128,128]{1,0:T(8,128)(2,1)S(1)}, u32[]{:S(2)}, u32[]{:S(2)}) collective-permute-start(bf16[128,128]{1,0:T(8,128)(2,1)S(1)} %get-tuple-element.50), channel_id=1, source_target_pairs={{0,248},{4,252},{8,0},{12,4},{16,8},{20,12},{24,16},{28,20},{32,24... | collective-permute-start | bytes 98312 | tf_op jit(solution)/shard_map/ppermute | solution.py:24
  64.4 4.5 %collective-permute-start.20 = (bf16[128,128]{1,0:T(8,128)(2,1)S(1)}, bf16[128,128]{1,0:T(8,128)(2,1)S(1)}, u32[]{:S(2)}, u32[]{:S(2)}) collective-permute-start(bf16[128,128]{1,0:T(8,128)(2,1)S(1)} %get-tuple-element.51), channel_id=1, source_target_pairs={{0,252},{4,0},{8,4},{12,8},{16,12},{20,16},{24,20},{28,24},{32,28}... | collective-permute-start | bytes 98312 | tf_op jit(solution)/shard_map/ppermute | solution.py:24
  64.8 5.5 %collective-permute-start.21 = (bf16[128,128]{1,0:T(8,128)(2,1)S(1)}, bf16[128,128]{1,0:T(8,128)(2,1)S(1)}, u32[]{:S(2)}, u32[]{:S(2)}) collective-permute-start(bf16[128,128]{1,0:T(8,128)(2,1)S(1)} %get-tuple-element.53), channel_id=1, source_target_pairs={{0,4},{4,8},{8,12},{12,16},{16,20},{20,24},{24,28},{28,32},{32,36}... | collective-permute-start | bytes 98312 | tf_op jit(solution)/shard_map/ppermute | solution.py:24
  66.2 7.2 %collective-permute-start.22 = (bf16[128,128]{1,0:T(8,128)(2,1)S(1)}, bf16[128,128]{1,0:T(8,128)(2,1)S(1)}, u32[]{:S(2)}, u32[]{:S(2)}) collective-permute-start(bf16[128,128]{1,0:T(8,128)(2,1)S(1)} %get-tuple-element.54), channel_id=1, source_target_pairs={{0,8},{4,12},{8,16},{12,20},{16,24},{20,28},{24,32},{28,36},{32,40... | collective-permute-start | bytes 98312 | tf_op jit(solution)/shard_map/ppermute | solution.py:24
  67.7 6.7 %collective-permute-start.23 = (bf16[128,128]{1,0:T(8,128)(2,1)S(1)}, bf16[128,128]{1,0:T(8,128)(2,1)S(1)}, u32[]{:S(2)}, u32[]{:S(2)}) collective-permute-start(bf16[128,128]{1,0:T(8,128)(2,1)S(1)} %get-tuple-element.55), channel_id=1, source_target_pairs={{0,12},{4,16},{8,20},{12,24},{16,28},{20,32},{24,36},{28,40},{32,4... | collective-permute-start | bytes 98312 | tf_op jit(solution)/shard_map/ppermute | solution.py:24
  69.0 17.3 %collective-permute-start.11 = (bf16[1024,128]{1,0:T(8,128)(2,1)S(1)}, bf16[1024,128]{1,0:T(8,128)(2,1)S(1)}, u32[]{:S(2)}, u32[]{:S(2)}) collective-permute-start(bf16[1024,128]{1,0:T(8,128)(2,1)S(1)} %get-tuple-element.44), channel_id=1, source_target_pairs={{0,3},{1,0},{2,1},{3,2},{4,7},{5,4},{6,5},{7,6},{8,11},{9,8},{10,9... | collective-permute-start | bytes 786440 | tf_op jit(solution)/shard_map/ppermute | solution.py:24
  70.3 16.0 %collective-permute-start.9 = (bf16[1024,128]{1,0:T(8,128)(2,1)S(1)}, bf16[1024,128]{1,0:T(8,128)(2,1)S(1)}, u32[]{:S(2)}, u32[]{:S(2)}) collective-permute-start(bf16[1024,128]{1,0:T(8,128)(2,1)S(1)} %get-tuple-element.42), channel_id=1, source_target_pairs={{0,1},{1,2},{2,3},{3,0},{4,5},{5,6},{6,7},{7,4},{8,9},{9,10},{10,1... | collective-permute-start | bytes 786440 | tf_op jit(solution)/shard_map/ppermute | solution.py:24
  73.4 7.0 %collective-permute-start.13 = (bf16[512,128]{1,0:T(8,128)(2,1)S(1)}, bf16[512,128]{1,0:T(8,128)(2,1)S(1)}, u32[]{:S(2)}, u32[]{:S(2)}) collective-permute-start(bf16[512,128]{1,0:T(8,128)(2,1)S(1)} %copy-done.5), channel_id=1, source_target_pairs={{0,2},{1,3},{2,0},{3,1},{4,6},{5,7},{6,4},{7,5},{8,10},{9,11},{10,... | collective-permute-start | bytes 393224 | tf_op jit(solution)/shard_map/ppermute | solution.py:24
  74.3 8.1 %collective-permute-start.14 = (bf16[512,128]{1,0:T(8,128)(2,1)S(1)}, bf16[512,128]{1,0:T(8,128)(2,1)S(1)}, u32[]{:S(2)}, u32[]{:S(2)}) collective-permute-start(bf16[512,128]{1,0:T(8,128)(2,1)S(1)} %copy-done.5), channel_id=1, source_target_pairs={{0,3},{1,0},{2,1},{3,2},{4,7},{5,4},{6,5},{7,6},{8,11},{9,8},{10,9... | collective-permute-start | bytes 393224 | tf_op jit(solution)/shard_map/ppermute | solution.py:24
  80.4 9.3 %collective-permute-start.24 = (bf16[640,128]{1,0:T(8,128)(2,1)S(1)}, bf16[640,128]{1,0:T(8,128)(2,1)S(1)}, u32[]{:S(2)}, u32[]{:S(2)}) collective-permute-start(bf16[640,128]{1,0:T(8,128)(2,1)S(1)} %get-tuple-element.57), channel_id=1, source_target_pairs={{0,1},{1,2},{2,3},{3,0},{4,5},{5,6},{6,7},{7,4},{8,9},{9,10},{10,1... | collective-permute-start | bytes 491528 | tf_op jit(solution)/shard_map/ppermute | solution.py:24
  82.4 9.3 %collective-permute-start.25 = (bf16[640,128]{1,0:T(8,128)(2,1)S(1)}, bf16[640,128]{1,0:T(8,128)(2,1)S(1)}, u32[]{:S(2)}, u32[]{:S(2)}) collective-permute-start(bf16[640,128]{1,0:T(8,128)(2,1)S(1)} %get-tuple-element.58), channel_id=1, source_target_pairs={{0,2},{1,3},{2,0},{3,1},{4,6},{5,7},{6,4},{7,5},{8,10},{9,11},{10,... | collective-permute-start | bytes 491528 | tf_op jit(solution)/shard_map/ppermute | solution.py:24
  83.8 9.6 %collective-permute-start.26 = (bf16[640,128]{1,0:T(8,128)(2,1)S(1)}, bf16[640,128]{1,0:T(8,128)(2,1)S(1)}, u32[]{:S(2)}, u32[]{:S(2)}) collective-permute-start(bf16[640,128]{1,0:T(8,128)(2,1)S(1)} %get-tuple-element.59), channel_id=1, source_target_pairs={{0,3},{1,0},{2,1},{3,2},{4,7},{5,4},{6,5},{7,6},{8,11},{9,8},{10,9... | collective-permute-start | bytes 491528 | tf_op jit(solution)/shard_map/ppermute | solution.py:24
  88.1 8.7 %collective-permute-start.15 = (bf16[1024,128]{1,0:T(8,128)(2,1)S(1)}, bf16[1024,128]{1,0:T(8,128)(2,1)S(1)}, u32[]{:S(2)}, u32[]{:S(2)}) collective-permute-start(bf16[1024,128]{1,0:T(8,128)(2,1)S(1)} %get-tuple-element.46), channel_id=1, source_target_pairs={{0,1},{1,2},{2,3},{3,0},{4,5},{5,6},{6,7},{7,4},{8,9},{9,10},{10,1... | collective-permute-start | bytes 786440 | tf_op jit(solution)/shard_map/ppermute | solution.py:24
  88.2 14.0 %collective-permute-start.16 = (bf16[1024,128]{1,0:T(8,128)(2,1)S(1)}, bf16[1024,128]{1,0:T(8,128)(2,1)S(1)}, u32[]{:S(2)}, u32[]{:S(2)}) collective-permute-start(bf16[1024,128]{1,0:T(8,128)(2,1)S(1)} %get-tuple-element.47), channel_id=1, source_target_pairs={{0,2},{1,3},{2,0},{3,1},{4,6},{5,7},{6,4},{7,5},{8,10},{9,11},{10,... | collective-permute-start | bytes 786440 | tf_op jit(solution)/shard_map/ppermute | solution.py:24
  89.7 14.9 %collective-permute-start.17 = (bf16[1024,128]{1,0:T(8,128)(2,1)S(1)}, bf16[1024,128]{1,0:T(8,128)(2,1)S(1)}, u32[]{:S(2)}, u32[]{:S(2)}) collective-permute-start(bf16[1024,128]{1,0:T(8,128)(2,1)S(1)} %get-tuple-element.48), channel_id=1, source_target_pairs={{0,3},{1,0},{2,1},{3,2},{4,7},{5,4},{6,5},{7,6},{8,11},{9,8},{10,9... | collective-permute-start | bytes 786440 | tf_op jit(solution)/shard_map/ppermute | solution.py:24
where the time goes:
time: 107 us; the launch traced here: 106 us
  starting transfers between devices  50.2 us (47%)
  Pallas kernels  24 us (22%)
  waiting for transfers between devices  20.5 us (19%)
  local copies, waits for them, and re-layouts  9.89 us (9%)
    ppermute x27, starting transfers between devices, ring(): lax.ppermute(shard, axis, [(i, (i + by) % devices) for i in range(devices)])  50.2 us
    pallas_call x7, Pallas kernels, call(): pl.pallas_call(kernel, out_shape=out_shape, cost_estimate=pl.CostEstimate...  24 us
    ppermute x27, waiting for transfers between devices, ring(): lax.ppermute(shard, axis, [(i, (i + by) % devices) for i in range(devices)])  20.5 us
    unnamed x18, local copies, waits for them, and re-layouts  8.28 us
  transfers between devices with their start and end apart: 27, of which 10 were waited for; matrix products, arithmetic and copies ran while one was open for 2% of the time, Pallas kernels for 19%

commit v1 on v0

--- a/solution.py
+++ b/solution.py
@@ -15,7 +15,7 @@
 WINDOW = 384
 ROWS = 1024
 OWN = 3
-OTHERS = (2, 4, 1, 5, 0, 6)
+OTHERS = (2, 1, 0, 4, 5, 6)
 ORDER = (OWN, *OTHERS)
 
 
@@ -251,10 +251,11 @@
         in_specs=[vmem] * 4,
         out_specs=[vmem] * span,
     )
+    arrived = [ring(picked[k], "band", OWN - k) for k in OTHERS]
     slots_here = call(
         join_kernel,
         shape((slot_count, 2 * LANES), BF16),
-        (picked[OWN], *[ring(picked[k], "band", OWN - k) for k in OTHERS]),
+        (picked[OWN], *arrived),
         0,
         8 * slot_count * LANES,
         4,
@@ -293,9 +294,9 @@
     )
     sums, slot_sums = result[:4], result[4:]
 
+    hidden_parts = [sums[0]] + from_peers(sums, True)
     back = {k: ring(slot_sums[k], "band", k - OWN) for k in OTHERS}
     back[OWN] = slot_sums[OWN]
-    hidden_parts = [sums[0]] + from_peers(sums, True)
     node_terms = call(
         node_kernel,
         [shape((nodes, LANES), F32)] + [shape((nodes, LANES), BF16)] * 3,
@@ -327,8 +328,9 @@
         in_specs=[smem] + [vmem] * 4,
         out_specs=vmem,
     )
+    node_parts = from_peers(node_terms, True)
     node_grad = node_terms[0]
-    for part in from_peers(node_terms, True):
+    for part in node_parts:
         node_grad = node_grad + part.astype(F32)
     return (grid_grad, node_grad.astype(BF16))
 

time: 107 us -> 104 us (0.972)
  starting transfers between devices: 50.2 us -> 43.2 us
  waiting for transfers between devices: 20.5 us -> 24.5 us
    ppermute x27, starting transfers between devices: 50.2 us -> 43.2 us  [ring(): lax.ppermute(shard, axis, [(i, (i + by) % devices) for i in range(devices)])]
    ppermute x27, waiting for transfers between devices: 20.5 us -> 24.5 us  [ring(): lax.ppermute(shard, axis, [(i, (i + by) % devices) for i in range(devices)])]
  transfers between devices with their start and end apart: 27 -> 27, of which waited for: 10 -> 11; matrix products, arithmetic and copies ran while one was open for 2% -> 2% of each run, Pallas kernels for 19% -> 20%
where the time goes in v1:
time: 104 us; the launch traced here: 103 us
  starting transfers between devices  43.2 us (42%)
  waiting for transfers between devices  24.5 us (24%)
  Pallas kernels  24.1 us (23%)
  local copies, waits for them, and re-layouts  9.89 us (10%)
    ppermute x27, starting transfers between devices, ring(): lax.ppermute(shard, axis, [(i, (i + by) % devices) for i in range(devices)])  43.2 us
    ppermute x27, waiting for transfers between devices, ring(): lax.ppermute(shard, axis, [(i, (i + by) % devices) for i in range(devices)])  24.5 us
    pallas_call x7, Pallas kernels, call(): pl.pallas_call(kernel, out_shape=out_shape, cost_estimate=pl.CostEstimate...  24.1 us
    unnamed x18, local copies, waits for them, and re-layouts  8.28 us
  transfers between devices with their start and end apart: 27, of which 11 were waited for; matrix products, arithmetic and copies ran while one was open for 2% of the time, Pallas kernels for 20%

profile of v1, /device:TPU:1, one launch (start us, length us, event | category | flops | bytes accessed | tf_op | source)
XLA Modules:
  0.0 103.3 jit_solution(4148122507705654706)
XLA Ops:
  0.6 2.3 %shard_map.140 = (bf16[128,256]{1,0:T(8,128)(2,1)}, bf16[128,256]{1,0:T(8,128)(2,1)}, bf16[128,256]{1,0:T(8,128)(2,1)}, bf16[128,256]{1,0:T(8,128)(2,1)}, bf16[1...) custom-call(bf16[640,128]{1,0:T(8,128)(2,1)} %lat_ref.2, bf16[640,128]{1,0:T(8,128)(2,1)} %grad_ref.1, ...), custom_call_target="tpu_custom_call" | custom-call | flops 293601280 | bytes 786432 | tf_op jit(solution)/shard_map/pallas_call | solution.py:58
  2.9 3.0 %collective-permute-start = (bf16[128,256]{1,0:T(8,128)(2,1)}, bf16[128,256]{1,0:T(8,128)(2,1)S(1)}, u32[]{:S(2)}, u32[]{:S(2)}) collective-permute-start(bf16[128,256]{1,0:T(8,128)(2,1)} %get-tuple-element.32), channel_id=1, source_target_pairs={{0,4},{4,8},{8,12},{12,16},{16,20},{20,24},{24,28},{28,32},{32,36}... | collective-permute-start | bytes 196616 | tf_op jit(solution)/shard_map/ppermute | solution.py:24
  5.9 1.6 %collective-permute-start.1 = (bf16[128,256]{1,0:T(8,128)(2,1)}, bf16[128,256]{1,0:T(8,128)(2,1)S(1)}, u32[]{:S(2)}, u32[]{:S(2)}) collective-permute-start(bf16[128,256]{1,0:T(8,128)(2,1)} %get-tuple-element.33), channel_id=1, source_target_pairs={{0,8},{4,12},{8,16},{12,20},{16,24},{20,28},{24,32},{28,36},{32,40... | collective-permute-start | bytes 196616 | tf_op jit(solution)/shard_map/ppermute | solution.py:24
  7.6 1.6 %collective-permute-start.2 = (bf16[128,256]{1,0:T(8,128)(2,1)}, bf16[128,256]{1,0:T(8,128)(2,1)S(1)}, u32[]{:S(2)}, u32[]{:S(2)}) collective-permute-start(bf16[128,256]{1,0:T(8,128)(2,1)} %get-tuple-element.34), channel_id=1, source_target_pairs={{0,12},{4,16},{8,20},{12,24},{16,28},{20,32},{24,36},{28,40},{32,4... | collective-permute-start | bytes 196616 | tf_op jit(solution)/shard_map/ppermute | solution.py:24
  9.6 3.1 %collective-permute-start.4 = (bf16[128,256]{1,0:T(8,128)(2,1)}, bf16[128,256]{1,0:T(8,128)(2,1)S(1)}, u32[]{:S(2)}, u32[]{:S(2)}) collective-permute-start(bf16[128,256]{1,0:T(8,128)(2,1)} %get-tuple-element.36), channel_id=1, source_target_pairs={{0,248},{4,252},{8,0},{12,4},{16,8},{20,12},{24,16},{28,20},{32,24... | collective-permute-start | bytes 196616 | tf_op jit(solution)/shard_map/ppermute | solution.py:24
  12.7 0.7 reshape.19.send_ref
  13.6 0.7 reshape.22.slot_ref
  14.4 3.1 %collective-permute-start.5 = (bf16[128,256]{1,0:T(8,128)(2,1)}, bf16[128,256]{1,0:T(8,128)(2,1)S(1)}, u32[]{:S(2)}, u32[]{:S(2)}) collective-permute-start(bf16[128,256]{1,0:T(8,128)(2,1)} %get-tuple-element.37), channel_id=1, source_target_pairs={{0,244},{4,248},{8,252},{12,0},{16,4},{20,8},{24,12},{28,16},{32,2... | collective-permute-start | bytes 196616 | tf_op jit(solution)/shard_map/ppermute | solution.py:24
  17.6 1.2 %collective-permute-start.12 = (bf16[512,128]{1,0:T(8,128)(2,1)}, bf16[512,128]{1,0:T(8,128)(2,1)S(1)}, u32[]{:S(2)}, u32[]{:S(2)}) collective-permute-start(bf16[512,128]{1,0:T(8,128)(2,1)} %refs_4_.3), channel_id=1, source_target_pairs={{0,1},{1,2},{2,3},{3,0},{4,5},{5,6},{6,7},{7,4},{8,9},{9,10},{10,1... | collective-permute-start | bytes 393224 | tf_op jit(solution)/shard_map/ppermute | solution.py:24
  18.8 1.6 %collective-permute-done.5.refs_6_ = bf16[128,256]{1,0:T(8,128)(2,1)S(1)} collective-permute-done((bf16[128,256]{1,0:T(8,128)(2,1)}, bf16[128,256]{1,0:T(8,128)(2,1)S(1)}, u32[]{:S(2)}, u32[]{:S(2)}) %collective-permute-start.5) | collective-permute-done | bytes 65568 | tf_op jit(solution)/shard_map/ppermute | solution.py:24
  20.5 0.8 copy-done.6
  21.4 1.3 %collective-permute-start.6 = (bf16[896,256]{1,0:T(8,128)(2,1)S(1)}, bf16[896,256]{1,0:T(8,128)(2,1)S(1)}, u32[]{:S(2)}, u32[]{:S(2)}) collective-permute-start(bf16[896,256]{1,0:T(8,128)(2,1)S(1)} %shard_map.141.refs_0_), channel_id=1, source_target_pairs={{0,1},{1,2},{2,3},{3,0},{4,5},{5,6},{6,7},{7,4},{8,9},{9,10},{10,1... | collective-permute-start | bytes 1376264 | tf_op jit(solution)/shard_map/ppermute | solution.py:24
  22.6 2.4 %collective-permute-start.7 = (bf16[896,256]{1,0:T(8,128)(2,1)S(1)}, bf16[896,256]{1,0:T(8,128)(2,1)S(1)}, u32[]{:S(2)}, u32[]{:S(2)}) collective-permute-start(bf16[896,256]{1,0:T(8,128)(2,1)S(1)} %shard_map.141.refs_0_), channel_id=1, source_target_pairs={{0,2},{1,3},{2,0},{3,1},{4,6},{5,7},{6,4},{7,5},{8,10},{9,11},{10,... | collective-permute-start | bytes 1376264 | tf_op jit(solution)/shard_map/ppermute | solution.py:24
  25.1 1.2 %collective-permute-start.8 = (bf16[896,256]{1,0:T(8,128)(2,1)S(1)}, bf16[896,256]{1,0:T(8,128)(2,1)S(1)}, u32[]{:S(2)}, u32[]{:S(2)}) collective-permute-start(bf16[896,256]{1,0:T(8,128)(2,1)S(1)} %shard_map.141.refs_0_), channel_id=1, source_target_pairs={{0,3},{1,0},{2,1},{3,2},{4,7},{5,4},{6,5},{7,6},{8,11},{9,8},{10,9... | collective-permute-start | bytes 1376264 | tf_op jit(solution)/shard_map/ppermute | solution.py:24
  26.3 2.8 %copy-done = bf16[6144,512]{1,0:T(8,128)(2,1)S(1)} copy-done((bf16[6144,512]{1,0:T(8,128)(2,1)S(1)}, bf16[6144,512]{1,0:T(8,128)(2,1)}, u32[]{:S(2)}) %copy-start) | copy-done | bytes 6291480
  29.1 2.2 %copy-done.1 = bf16[4096,512]{1,0:T(8,128)(2,1)S(1)} copy-done((bf16[4096,512]{1,0:T(8,128)(2,1)S(1)}, bf16[4096,512]{1,0:T(8,128)(2,1)}, u32[]{:S(2)}) %copy-start.1) | copy-done | bytes 4194328
  31.2 0.9 copy-done.2
  32.1 0.9 copy-done.5
  33.1 0.7 copy-done.7
  33.7 7.1 %shard_map.142 = (f32[6144,128]{1,0:T(8,128)S(1)}, bf16[6144,896]{1,0:T(8,128)(2,1)S(1)}, bf16[6144,384]{1,0:T(8,128)(2,1)S(1)}) custom-call(s32[24]{0:T(128)S(1)} %multiply_minimum_fusion.base_ref, bf16[4096,512]{1,0:T(8,128)(2,1)S(1)} %copy-done.1, bf16[6144,512]{1,0:T(8,128)(2,1)S(1)} %copy-done, s32[24,256]{1,0:T(8,128)S(1)} %reshape.19.send_ref, ...), custom_call_target="tpu_custom_call" | custom-call | flops 2550136832 | bytes 13631488 | tf_op jit(solution)/shard_map/pallas_call | solution.py:58
  40.9 3.8 %collective-permute-done.7.refs_2_ = bf16[896,256]{1,0:T(8,128)(2,1)S(1)} collective-permute-done((bf16[896,256]{1,0:T(8,128)(2,1)S(1)}, bf16[896,256]{1,0:T(8,128)(2,1)S(1)}, u32[]{:S(2)}, u32[]{:S(2)}) %collective-permute-start.7) | collective-permute-done | bytes 458784 | tf_op jit(solution)/shard_map/ppermute | solution.py:24
  44.7 9.5 %shard_map.143 = (bf16[1024,128]{1,0:T(8,128)(2,1)S(1)}, bf16[1024,128]{1,0:T(8,128)(2,1)S(1)}, bf16[1024,128]{1,0:T(8,128)(2,1)S(1)}, bf16[1024,128]{1,0:T(8,12...) custom-call(s32[24]{0:T(128)S(1)} %multiply_minimum_fusion.base_ref,, ...), custom_call_target="tpu_custom_call" | custom-call | flops 4831838208 | bytes 3145728 | tf_op jit(solution)/shard_map/pallas_call | solution.py:58
  54.2 2.2 %collective-permute-start.10 = (bf16[1024,128]{1,0:T(8,128)(2,1)S(1)}, bf16[1024,128]{1,0:T(8,128)(2,1)S(1)}, u32[]{:S(2)}, u32[]{:S(2)}) collective-permute-start(bf16[1024,128]{1,0:T(8,128)(2,1)S(1)} %get-tuple-element.43), channel_id=1, source_target_pairs={{0,2},{1,3},{2,0},{3,1},{4,6},{5,7},{6,4},{7,5},{8,10},{9,11},{10,... | collective-permute-start | bytes 786440 | tf_op jit(solution)/shard_map/ppermute | solution.py:24
  56.4 7.0 %collective-permute-start.18 = (bf16[128,128]{1,0:T(8,128)(2,1)S(1)}, bf16[128,128]{1,0:T(8,128)(2,1)S(1)}, u32[]{:S(2)}, u32[]{:S(2)}) collective-permute-start(bf16[128,128]{1,0:T(8,128)(2,1)S(1)} %get-tuple-element.49), channel_id=1, source_target_pairs={{0,244},{4,248},{8,252},{12,0},{16,4},{20,8},{24,12},{28,16},{32,2... | collective-permute-start | bytes 98312 | tf_op jit(solution)/shard_map/ppermute | solution.py:24
  63.4 0.4 collective-permute-start.20
  63.8 1.4 %collective-permute-start.21 = (bf16[128,128]{1,0:T(8,128)(2,1)S(1)}, bf16[128,128]{1,0:T(8,128)(2,1)S(1)}, u32[]{:S(2)}, u32[]{:S(2)}) collective-permute-start(bf16[128,128]{1,0:T(8,128)(2,1)S(1)} %get-tuple-element.53), channel_id=1, source_target_pairs={{0,4},{4,8},{8,12},{12,16},{16,20},{20,24},{24,28},{28,32},{32,36}... | collective-permute-start | bytes 98312 | tf_op jit(solution)/shard_map/ppermute | solution.py:24
  65.1 1.5 %collective-permute-start.22 = (bf16[128,128]{1,0:T(8,128)(2,1)S(1)}, bf16[128,128]{1,0:T(8,128)(2,1)S(1)}, u32[]{:S(2)}, u32[]{:S(2)}) collective-permute-start(bf16[128,128]{1,0:T(8,128)(2,1)S(1)} %get-tuple-element.54), channel_id=1, source_target_pairs={{0,8},{4,12},{8,16},{12,20},{16,24},{20,28},{24,32},{28,36},{32,40... | collective-permute-start | bytes 98312 | tf_op jit(solution)/shard_map/ppermute | solution.py:24
  66.7 1.1 %collective-permute-start.11 = (bf16[1024,128]{1,0:T(8,128)(2,1)S(1)}, bf16[1024,128]{1,0:T(8,128)(2,1)S(1)}, u32[]{:S(2)}, u32[]{:S(2)}) collective-permute-start(bf16[1024,128]{1,0:T(8,128)(2,1)S(1)} %get-tuple-element.44), channel_id=1, source_target_pairs={{0,3},{1,0},{2,1},{3,2},{4,7},{5,4},{6,5},{7,6},{8,11},{9,8},{10,9... | collective-permute-start | bytes 786440 | tf_op jit(solution)/shard_map/ppermute | solution.py:24
  67.8 0.4 collective-permute-start.9
  68.2 3.0 %collective-permute-done.22.refs_5_ = bf16[128,128]{1,0:T(8,128)(2,1)S(1)} collective-permute-done((bf16[128,128]{1,0:T(8,128)(2,1)S(1)}, bf16[128,128]{1,0:T(8,128)(2,1)S(1)}, u32[]{:S(2)}, u32[]{:S(2)}) %collective-permute-start.22) | collective-permute-done | bytes 32800 | tf_op jit(solution)/shard_map/ppermute | solution.py:24
  71.2 0.6 collective-permute-start.13
  71.8 1.6 %collective-permute-done.23.refs_6_ = bf16[128,128]{1,0:T(8,128)(2,1)S(1)} collective-permute-done((bf16[128,128]{1,0:T(8,128)(2,1)S(1)}, bf16[128,128]{1,0:T(8,128)(2,1)S(1)}, u32[]{:S(2)}, u32[]{:S(2)}) %collective-permute-start.23) | collective-permute-done | bytes 32800 | tf_op jit(solution)/shard_map/ppermute | solution.py:24
  73.4 1.4 %collective-permute-start.14 = (bf16[512,128]{1,0:T(8,128)(2,1)S(1)}, bf16[512,128]{1,0:T(8,128)(2,1)S(1)}, u32[]{:S(2)}, u32[]{:S(2)}) collective-permute-start(bf16[512,128]{1,0:T(8,128)(2,1)S(1)} %copy-done.5), channel_id=1, source_target_pairs={{0,3},{1,0},{2,1},{3,2},{4,7},{5,4},{6,5},{7,6},{8,11},{9,8},{10,9... | collective-permute-start | bytes 393224 | tf_op jit(solution)/shard_map/ppermute | solution.py:24
  74.8 1.8 %shard_map.146 = (f32[640,128]{1,0:T(8,128)S(1)}, bf16[640,128]{1,0:T(8,128)(2,1)S(1)}, bf16[640,128]{1,0:T(8,128)(2,1)S(1)}, bf16[640,128]{1,0:T(8,128)(2,1)S(1)}) custom-call(s32[8]{0:T(128)S(1)} %add_multiply_fusion.chan_ref, s32[7,1,128]{2,1,0:T(1,128)S(1)} %bitcast.5, bf16[512,128]{1,0:T(8,128)(2,1)S(1)} %copy-done.4, ...), custom_call_target="tpu_custom_call" | custom-call | flops 314572800 | bytes 655360 | tf_op jit(solution)/shard_map/pallas_call | solution.py:58
  76.6 1.4 %collective-permute-done.13.refs_6_ = bf16[512,128]{1,0:T(8,128)(2,1)S(1)} collective-permute-done((bf16[512,128]{1,0:T(8,128)(2,1)S(1)}, bf16[512,128]{1,0:T(8,128)(2,1)S(1)}, u32[]{:S(2)}, u32[]{:S(2)}) %collective-permute-start.13) | collective-permute-done | bytes 131104 | tf_op jit(solution)/shard_map/ppermute | solution.py:24
  77.9 0.6 collective-permute-start.24
  78.6 1.0 collective-permute-done.14.refs_7_
  79.6 2.4 %collective-permute-start.25 = (bf16[640,128]{1,0:T(8,128)(2,1)S(1)}, bf16[640,128]{1,0:T(8,128)(2,1)S(1)}, u32[]{:S(2)}, u32[]{:S(2)}) collective-permute-start(bf16[640,128]{1,0:T(8,128)(2,1)S(1)} %get-tuple-element.58), channel_id=1, source_target_pairs={{0,2},{1,3},{2,0},{3,1},{4,6},{5,7},{6,4},{7,5},{8,10},{9,11},{10,... | collective-permute-start | bytes 491528 | tf_op jit(solution)/shard_map/ppermute | solution.py:24
  82.0 2.0 %collective-permute-start.26 = (bf16[640,128]{1,0:T(8,128)(2,1)S(1)}, bf16[640,128]{1,0:T(8,128)(2,1)S(1)}, u32[]{:S(2)}, u32[]{:S(2)}) collective-permute-start(bf16[640,128]{1,0:T(8,128)(2,1)S(1)} %get-tuple-element.59), channel_id=1, source_target_pairs={{0,3},{1,0},{2,1},{3,2},{4,7},{5,4},{6,5},{7,6},{8,11},{9,8},{10,9... | collective-permute-start | bytes 491528 | tf_op jit(solution)/shard_map/ppermute | solution.py:24
  84.0 1.8 %shard_map.144 = (bf16[1024,128]{1,0:T(8,128)(2,1)S(1)}, bf16[1024,128]{1,0:T(8,128)(2,1)S(1)}, bf16[1024,128]{1,0:T(8,128)(2,1)S(1)}, bf16[1024,128]{1,0:T(8,128)(2,1)S(1)}) custom-call(s32[8]{0:T(128)S(1)} %add_multiply_fusion.chan_ref, bf16[1024,128]{1,0:T(8,128)(2,1)S(1)} %get-tuple-element.41.refs_0_, ...), custom_call_target="tpu_custom_call" | custom-call | flops 536870912 | bytes 2097152 | tf_op jit(solution)/shard_map/pallas_call | solution.py:58
  85.9 1.2 %collective-permute-start.16 = (bf16[1024,128]{1,0:T(8,128)(2,1)S(1)}, bf16[1024,128]{1,0:T(8,128)(2,1)S(1)}, u32[]{:S(2)}, u32[]{:S(2)}) collective-permute-start(bf16[1024,128]{1,0:T(8,128)(2,1)S(1)} %get-tuple-element.47), channel_id=1, source_target_pairs={{0,2},{1,3},{2,0},{3,1},{4,6},{5,7},{6,4},{7,5},{8,10},{9,11},{10,... | collective-permute-start | bytes 786440 | tf_op jit(solution)/shard_map/ppermute | solution.py:24
  87.1 2.0 %collective-permute-start.17 = (bf16[1024,128]{1,0:T(8,128)(2,1)S(1)}, bf16[1024,128]{1,0:T(8,128)(2,1)S(1)}, u32[]{:S(2)}, u32[]{:S(2)}) collective-permute-start(bf16[1024,128]{1,0:T(8,128)(2,1)S(1)} %get-tuple-element.48), channel_id=1, source_target_pairs={{0,3},{1,0},{2,1},{3,2},{4,7},{5,4},{6,5},{7,6},{8,11},{9,8},{10,9... | collective-permute-start | bytes 786440 | tf_op jit(solution)/shard_map/ppermute | solution.py:24
  89.0 2.0 %collective-permute-done.26 = bf16[640,128]{1,0:T(8,128)(2,1)S(1)} collective-permute-done((bf16[640,128]{1,0:T(8,128)(2,1)S(1)}, bf16[640,128]{1,0:T(8,128)(2,1)S(1)}, u32[]{:S(2)}, u32[]{:S(2)}) %collective-permute-start.26) | collective-permute-done | bytes 163872 | tf_op jit(solution)/shard_map/ppermute | solution.py:24
  91.0 0.7 add_convert_fusion
  91.8 1.9 %collective-permute-done.15.refs_1_ = bf16[1024,128]{1,0:T(8,128)(2,1)S(1)} collective-permute-done((bf16[1024,128]{1,0:T(8,128)(2,1)S(1)}, bf16[1024,128]{1,0:T(8,128)(2,1)S(1)}, u32[]{:S(2)}, u32[]{:S(2)}) %collective-permute-start.15) | collective-permute-done | bytes 262176 | tf_op jit(solution)/shard_map/ppermute | solution.py:24
  93.7 5.9 %collective-permute-done.16.refs_2_ = bf16[1024,128]{1,0:T(8,128)(2,1)S(1)} collective-permute-done((bf16[1024,128]{1,0:T(8,128)(2,1)S(1)}, bf16[1024,128]{1,0:T(8,128)(2,1)S(1)}, u32[]{:S(2)}, u32[]{:S(2)}) %collective-permute-start.16) | collective-permute-done | bytes 262176 | tf_op jit(solution)/shard_map/ppermute | solution.py:24
  99.6 2.1 %collective-permute-done.17.refs_3_ = bf16[1024,128]{1,0:T(8,128)(2,1)S(1)} collective-permute-done((bf16[1024,128]{1,0:T(8,128)(2,1)S(1)}, bf16[1024,128]{1,0:T(8,128)(2,1)S(1)}, u32[]{:S(2)}, u32[]{:S(2)}) %collective-permute-start.17) | collective-permute-done | bytes 262176 | tf_op jit(solution)/shard_map/ppermute | solution.py:24
  101.7 1.6 %shard_map.145 = bf16[4096,128]{1,0:T(8,128)(2,1)} custom-call(s32[8]{0:T(128)S(1)} %add_multiply_fusion.chan_ref, bf16[1024,128]{1,0:T(8,128)(2,1)S(1)} %get-tuple-element.45.refs_0_, bf16[1024,128]{1,0:T(8,128)(2,1)S(1)} %collective-permute-done.15.refs_1_, bf16[1024,128]{1,0:T(8,128)(2,1)S(1)} %collective-permute-done.16.refs_2_, ...), custom_call_target="tpu_custom_call" | custom-call | bytes 2097152 | tf_op jit(solution)/shard_map/pallas_call | solution.py:58
  (38 shorter events, 0.9 us)
Async XLA Ops:
  2.9 11.5 %collective-permute-start = (bf16[128,256]{1,0:T(8,128)(2,1)}, bf16[128,256]{1,0:T(8,128)(2,1)S(1)}, u32[]{:S(2)}, u32[]{:S(2)}) collective-permute-start(bf16[128,256]{1,0:T(8,128)(2,1)} %get-tuple-element.32), channel_id=1, source_target_pairs={{0,4},{4,8},{8,12},{12,16},{16,20},{20,24},{24,28},{28,32},{32,36}... | collective-permute-start | bytes 196616 | tf_op jit(solution)/shard_map/ppermute | solution.py:24
  5.9 11.7 %collective-permute-start.1 = (bf16[128,256]{1,0:T(8,128)(2,1)}, bf16[128,256]{1,0:T(8,128)(2,1)S(1)}, u32[]{:S(2)}, u32[]{:S(2)}) collective-permute-start(bf16[128,256]{1,0:T(8,128)(2,1)} %get-tuple-element.33), channel_id=1, source_target_pairs={{0,8},{4,12},{8,16},{12,20},{16,24},{20,28},{24,32},{28,36},{32,40... | collective-permute-start | bytes 196616 | tf_op jit(solution)/shard_map/ppermute | solution.py:24
  7.6 11.3 %collective-permute-start.2 = (bf16[128,256]{1,0:T(8,128)(2,1)}, bf16[128,256]{1,0:T(8,128)(2,1)S(1)}, u32[]{:S(2)}, u32[]{:S(2)}) collective-permute-start(bf16[128,256]{1,0:T(8,128)(2,1)} %get-tuple-element.34), channel_id=1, source_target_pairs={{0,12},{4,16},{8,20},{12,24},{16,28},{20,32},{24,36},{28,40},{32,4... | collective-permute-start | bytes 196616 | tf_op jit(solution)/shard_map/ppermute | solution.py:24
  9.2 9.6 %collective-permute-start.3 = (bf16[128,256]{1,0:T(8,128)(2,1)}, bf16[128,256]{1,0:T(8,128)(2,1)S(1)}, u32[]{:S(2)}, u32[]{:S(2)}) collective-permute-start(bf16[128,256]{1,0:T(8,128)(2,1)} %get-tuple-element.35), channel_id=1, source_target_pairs={{0,252},{4,0},{8,4},{12,8},{16,12},{20,16},{24,20},{28,24},{32,28}... | collective-permute-start | bytes 196616 | tf_op jit(solution)/shard_map/ppermute | solution.py:24
  9.6 9.2 %collective-permute-start.4 = (bf16[128,256]{1,0:T(8,128)(2,1)}, bf16[128,256]{1,0:T(8,128)(2,1)S(1)}, u32[]{:S(2)}, u32[]{:S(2)}) collective-permute-start(bf16[128,256]{1,0:T(8,128)(2,1)} %get-tuple-element.36), channel_id=1, source_target_pairs={{0,248},{4,252},{8,0},{12,4},{16,8},{20,12},{24,16},{28,20},{32,24... | collective-permute-start | bytes 196616 | tf_op jit(solution)/shard_map/ppermute | solution.py:24
  14.4 6.1 %collective-permute-start.5 = (bf16[128,256]{1,0:T(8,128)(2,1)}, bf16[128,256]{1,0:T(8,128)(2,1)S(1)}, u32[]{:S(2)}, u32[]{:S(2)}) collective-permute-start(bf16[128,256]{1,0:T(8,128)(2,1)} %get-tuple-element.37), channel_id=1, source_target_pairs={{0,244},{4,248},{8,252},{12,0},{16,4},{20,8},{24,12},{28,16},{32,2... | collective-permute-start | bytes 196616 | tf_op jit(solution)/shard_map/ppermute | solution.py:24
  17.6 46.2 %collective-permute-start.12 = (bf16[512,128]{1,0:T(8,128)(2,1)}, bf16[512,128]{1,0:T(8,128)(2,1)S(1)}, u32[]{:S(2)}, u32[]{:S(2)}) collective-permute-start(bf16[512,128]{1,0:T(8,128)(2,1)} %refs_4_.3), channel_id=1, source_target_pairs={{0,1},{1,2},{2,3},{3,0},{4,5},{5,6},{6,7},{7,4},{8,9},{9,10},{10,1... | collective-permute-start | bytes 393224 | tf_op jit(solution)/shard_map/ppermute | solution.py:24
  20.5 0.8 copy-start.6
  21.4 19.5 %collective-permute-start.6 = (bf16[896,256]{1,0:T(8,128)(2,1)S(1)}, bf16[896,256]{1,0:T(8,128)(2,1)S(1)}, u32[]{:S(2)}, u32[]{:S(2)}) collective-permute-start(bf16[896,256]{1,0:T(8,128)(2,1)S(1)} %shard_map.141.refs_0_), channel_id=1, source_target_pairs={{0,1},{1,2},{2,3},{3,0},{4,5},{5,6},{6,7},{7,4},{8,9},{9,10},{10,1... | collective-permute-start | bytes 1376264 | tf_op jit(solution)/shard_map/ppermute | solution.py:24
  22.6 22.0 %collective-permute-start.7 = (bf16[896,256]{1,0:T(8,128)(2,1)S(1)}, bf16[896,256]{1,0:T(8,128)(2,1)S(1)}, u32[]{:S(2)}, u32[]{:S(2)}) collective-permute-start(bf16[896,256]{1,0:T(8,128)(2,1)S(1)} %shard_map.141.refs_0_), channel_id=1, source_target_pairs={{0,2},{1,3},{2,0},{3,1},{4,6},{5,7},{6,4},{7,5},{8,10},{9,11},{10,... | collective-permute-start | bytes 1376264 | tf_op jit(solution)/shard_map/ppermute | solution.py:24
  25.1 19.6 %collective-permute-start.8 = (bf16[896,256]{1,0:T(8,128)(2,1)S(1)}, bf16[896,256]{1,0:T(8,128)(2,1)S(1)}, u32[]{:S(2)}, u32[]{:S(2)}) collective-permute-start(bf16[896,256]{1,0:T(8,128)(2,1)S(1)} %shard_map.141.refs_0_), channel_id=1, source_target_pairs={{0,3},{1,0},{2,1},{3,2},{4,7},{5,4},{6,5},{7,6},{8,11},{9,8},{10,9... | collective-permute-start | bytes 1376264 | tf_op jit(solution)/shard_map/ppermute | solution.py:24
  26.3 2.8 %copy-start = (bf16[6144,512]{1,0:T(8,128)(2,1)S(1)}, bf16[6144,512]{1,0:T(8,128)(2,1)}, u32[]{:S(2)}) copy-start(bf16[6144,512]{1,0:T(8,128)(2,1)} %edge_ref.1) | copy-start | bytes 18874372
  29.1 2.2 %copy-start.1 = (bf16[4096,512]{1,0:T(8,128)(2,1)S(1)}, bf16[4096,512]{1,0:T(8,128)(2,1)}, u32[]{:S(2)}) copy-start(bf16[4096,512]{1,0:T(8,128)(2,1)} %lat_ref.3) | copy-start | bytes 12582916
  31.2 0.9 copy-start.2
  32.1 0.9 copy-start.5
  33.1 0.7 copy-start.7
  33.7 11.0 %copy-start.3 = (bf16[128,512]{1,0:T(8,128)(2,1)S(1)}, bf16[128,512]{1,0:T(8,128)(2,1)}, u32[]{:S(2)}) copy-start(bf16[128,512]{1,0:T(8,128)(2,1)} %refs_5_.1) | copy-start | bytes 393220
  33.7 11.0 %copy-start.4 = (bf16[512,128]{1,0:T(8,128)(2,1)S(1)}, bf16[512,128]{1,0:T(8,128)(2,1)}, u32[]{:S(2)}) copy-start(bf16[512,128]{1,0:T(8,128)(2,1)} %recv_ref.1) | copy-start | bytes 393220
  44.7 30.1 %copy-start.8 = (s32[1,7,128]{2,0,1:T(1,128)S(1)}, s32[1,7,128]{2,0,1:T(1,128)}, u32[]{:S(2)}) copy-start(s32[1,7,128]{2,0,1:T(1,128)} %param.18) | copy-start | bytes 10756
  54.2 27.8 %collective-permute-start.10 = (bf16[1024,128]{1,0:T(8,128)(2,1)S(1)}, bf16[1024,128]{1,0:T(8,128)(2,1)S(1)}, u32[]{:S(2)}, u32[]{:S(2)}) collective-permute-start(bf16[1024,128]{1,0:T(8,128)(2,1)S(1)} %get-tuple-element.43), channel_id=1, source_target_pairs={{0,2},{1,3},{2,0},{3,1},{4,6},{5,7},{6,4},{7,5},{8,10},{9,11},{10,... | collective-permute-start | bytes 786440 | tf_op jit(solution)/shard_map/ppermute | solution.py:24
  56.4 8.7 %collective-permute-start.18 = (bf16[128,128]{1,0:T(8,128)(2,1)S(1)}, bf16[128,128]{1,0:T(8,128)(2,1)S(1)}, u32[]{:S(2)}, u32[]{:S(2)}) collective-permute-start(bf16[128,128]{1,0:T(8,128)(2,1)S(1)} %get-tuple-element.49), channel_id=1, source_target_pairs={{0,244},{4,248},{8,252},{12,0},{16,4},{20,8},{24,12},{28,16},{32,2... | collective-permute-start | bytes 98312 | tf_op jit(solution)/shard_map/ppermute | solution.py:24
  63.4 3.2 %collective-permute-start.19 = (bf16[128,128]{1,0:T(8,128)(2,1)S(1)}, bf16[128,128]{1,0:T(8,128)(2,1)S(1)}, u32[]{:S(2)}, u32[]{:S(2)}) collective-permute-start(bf16[128,128]{1,0:T(8,128)(2,1)S(1)} %get-tuple-element.50), channel_id=1, source_target_pairs={{0,248},{4,252},{8,0},{12,4},{16,8},{20,12},{24,16},{28,20},{32,24... | collective-permute-start | bytes 98312 | tf_op jit(solution)/shard_map/ppermute | solution.py:24
  63.4 3.3 %collective-permute-start.20 = (bf16[128,128]{1,0:T(8,128)(2,1)S(1)}, bf16[128,128]{1,0:T(8,128)(2,1)S(1)}, u32[]{:S(2)}, u32[]{:S(2)}) collective-permute-start(bf16[128,128]{1,0:T(8,128)(2,1)S(1)} %get-tuple-element.51), channel_id=1, source_target_pairs={{0,252},{4,0},{8,4},{12,8},{16,12},{20,16},{24,20},{28,24},{32,28}... | collective-permute-start | bytes 98312 | tf_op jit(solution)/shard_map/ppermute | solution.py:24
  63.8 4.0 %collective-permute-start.21 = (bf16[128,128]{1,0:T(8,128)(2,1)S(1)}, bf16[128,128]{1,0:T(8,128)(2,1)S(1)}, u32[]{:S(2)}, u32[]{:S(2)}) collective-permute-start(bf16[128,128]{1,0:T(8,128)(2,1)S(1)} %get-tuple-element.53), channel_id=1, source_target_pairs={{0,4},{4,8},{8,12},{12,16},{16,20},{20,24},{24,28},{28,32},{32,36}... | collective-permute-start | bytes 98312 | tf_op jit(solution)/shard_map/ppermute | solution.py:24
  65.1 6.1 %collective-permute-start.22 = (bf16[128,128]{1,0:T(8,128)(2,1)S(1)}, bf16[128,128]{1,0:T(8,128)(2,1)S(1)}, u32[]{:S(2)}, u32[]{:S(2)}) collective-permute-start(bf16[128,128]{1,0:T(8,128)(2,1)S(1)} %get-tuple-element.54), channel_id=1, source_target_pairs={{0,8},{4,12},{8,16},{12,20},{16,24},{20,28},{24,32},{28,36},{32,40... | collective-permute-start | bytes 98312 | tf_op jit(solution)/shard_map/ppermute | solution.py:24
  66.6 6.8 %collective-permute-start.23 = (bf16[128,128]{1,0:T(8,128)(2,1)S(1)}, bf16[128,128]{1,0:T(8,128)(2,1)S(1)}, u32[]{:S(2)}, u32[]{:S(2)}) collective-permute-start(bf16[128,128]{1,0:T(8,128)(2,1)S(1)} %get-tuple-element.55), channel_id=1, source_target_pairs={{0,12},{4,16},{8,20},{12,24},{16,28},{20,32},{24,36},{28,40},{32,4... | collective-permute-start | bytes 98312 | tf_op jit(solution)/shard_map/ppermute | solution.py:24
  66.7 17.3 %collective-permute-start.11 = (bf16[1024,128]{1,0:T(8,128)(2,1)S(1)}, bf16[1024,128]{1,0:T(8,128)(2,1)S(1)}, u32[]{:S(2)}, u32[]{:S(2)}) collective-permute-start(bf16[1024,128]{1,0:T(8,128)(2,1)S(1)} %get-tuple-element.44), channel_id=1, source_target_pairs={{0,3},{1,0},{2,1},{3,2},{4,7},{5,4},{6,5},{7,6},{8,11},{9,8},{10,9... | collective-permute-start | bytes 786440 | tf_op jit(solution)/shard_map/ppermute | solution.py:24
  67.8 16.2 %collective-permute-start.9 = (bf16[1024,128]{1,0:T(8,128)(2,1)S(1)}, bf16[1024,128]{1,0:T(8,128)(2,1)S(1)}, u32[]{:S(2)}, u32[]{:S(2)}) collective-permute-start(bf16[1024,128]{1,0:T(8,128)(2,1)S(1)} %get-tuple-element.42), channel_id=1, source_target_pairs={{0,1},{1,2},{2,3},{3,0},{4,5},{5,6},{6,7},{7,4},{8,9},{9,10},{10,1... | collective-permute-start | bytes 786440 | tf_op jit(solution)/shard_map/ppermute | solution.py:24
  71.2 6.7 %collective-permute-start.13 = (bf16[512,128]{1,0:T(8,128)(2,1)S(1)}, bf16[512,128]{1,0:T(8,128)(2,1)S(1)}, u32[]{:S(2)}, u32[]{:S(2)}) collective-permute-start(bf16[512,128]{1,0:T(8,128)(2,1)S(1)} %copy-done.5), channel_id=1, source_target_pairs={{0,2},{1,3},{2,0},{3,1},{4,6},{5,7},{6,4},{7,5},{8,10},{9,11},{10,... | collective-permute-start | bytes 393224 | tf_op jit(solution)/shard_map/ppermute | solution.py:24
  73.4 6.2 %collective-permute-start.14 = (bf16[512,128]{1,0:T(8,128)(2,1)S(1)}, bf16[512,128]{1,0:T(8,128)(2,1)S(1)}, u32[]{:S(2)}, u32[]{:S(2)}) collective-permute-start(bf16[512,128]{1,0:T(8,128)(2,1)S(1)} %copy-done.5), channel_id=1, source_target_pairs={{0,3},{1,0},{2,1},{3,2},{4,7},{5,4},{6,5},{7,6},{8,11},{9,8},{10,9... | collective-permute-start | bytes 393224 | tf_op jit(solution)/shard_map/ppermute | solution.py:24
  77.9 9.1 %collective-permute-start.24 = (bf16[640,128]{1,0:T(8,128)(2,1)S(1)}, bf16[640,128]{1,0:T(8,128)(2,1)S(1)}, u32[]{:S(2)}, u32[]{:S(2)}) collective-permute-start(bf16[640,128]{1,0:T(8,128)(2,1)S(1)} %get-tuple-element.57), channel_id=1, source_target_pairs={{0,1},{1,2},{2,3},{3,0},{4,5},{5,6},{6,7},{7,4},{8,9},{9,10},{10,1... | collective-permute-start | bytes 491528 | tf_op jit(solution)/shard_map/ppermute | solution.py:24
  79.6 9.5 %collective-permute-start.25 = (bf16[640,128]{1,0:T(8,128)(2,1)S(1)}, bf16[640,128]{1,0:T(8,128)(2,1)S(1)}, u32[]{:S(2)}, u32[]{:S(2)}) collective-permute-start(bf16[640,128]{1,0:T(8,128)(2,1)S(1)} %get-tuple-element.58), channel_id=1, source_target_pairs={{0,2},{1,3},{2,0},{3,1},{4,6},{5,7},{6,4},{7,5},{8,10},{9,11},{10,... | collective-permute-start | bytes 491528 | tf_op jit(solution)/shard_map/ppermute | solution.py:24
  82.0 9.0 %collective-permute-start.26 = (bf16[640,128]{1,0:T(8,128)(2,1)S(1)}, bf16[640,128]{1,0:T(8,128)(2,1)S(1)}, u32[]{:S(2)}, u32[]{:S(2)}) collective-permute-start(bf16[640,128]{1,0:T(8,128)(2,1)S(1)} %get-tuple-element.59), channel_id=1, source_target_pairs={{0,3},{1,0},{2,1},{3,2},{4,7},{5,4},{6,5},{7,6},{8,11},{9,8},{10,9... | collective-permute-start | bytes 491528 | tf_op jit(solution)/shard_map/ppermute | solution.py:24
  85.8 8.0 %collective-permute-start.15 = (bf16[1024,128]{1,0:T(8,128)(2,1)S(1)}, bf16[1024,128]{1,0:T(8,128)(2,1)S(1)}, u32[]{:S(2)}, u32[]{:S(2)}) collective-permute-start(bf16[1024,128]{1,0:T(8,128)(2,1)S(1)} %get-tuple-element.46), channel_id=1, source_target_pairs={{0,1},{1,2},{2,3},{3,0},{4,5},{5,6},{6,7},{7,4},{8,9},{9,10},{10,1... | collective-permute-start | bytes 786440 | tf_op jit(solution)/shard_map/ppermute | solution.py:24
  85.9 13.7 %collective-permute-start.16 = (bf16[1024,128]{1,0:T(8,128)(2,1)S(1)}, bf16[1024,128]{1,0:T(8,128)(2,1)S(1)}, u32[]{:S(2)}, u32[]{:S(2)}) collective-permute-start(bf16[1024,128]{1,0:T(8,128)(2,1)S(1)} %get-tuple-element.47), channel_id=1, source_target_pairs={{0,2},{1,3},{2,0},{3,1},{4,6},{5,7},{6,4},{7,5},{8,10},{9,11},{10,... | collective-permute-start | bytes 786440 | tf_op jit(solution)/shard_map/ppermute | solution.py:24
  87.1 14.6 %collective-permute-start.17 = (bf16[1024,128]{1,0:T(8,128)(2,1)S(1)}, bf16[1024,128]{1,0:T(8,128)(2,1)S(1)}, u32[]{:S(2)}, u32[]{:S(2)}) collective-permute-start(bf16[1024,128]{1,0:T(8,128)(2,1)S(1)} %get-tuple-element.48), channel_id=1, source_target_pairs={{0,3},{1,0},{2,1},{3,2},{4,7},{5,4},{6,5},{7,6},{8,11},{9,8},{10,9... | collective-permute-start | bytes 786440 | tf_op jit(solution)/shard_map/ppermute | solution.py:24
